TPU v7x, 128 devices: a whole 4x4x4 slice. The times are simulated.
128 devices in a mesh: stage: 1, data: 128 (over z, y, x, core).
Axes of the slice: x: 4, y: 4, z: 4, core: 2. Of those that a mesh axis runs over, the one named last changes fastest.
Arguments:
- grad_attn: float32 [128, 1, 1024, 1024], P(('stage', 'data'))
- mom_attn: float32 [1, 1024, 1024], P('stage', 'data')
- master_attn: float32 [1, 1024, 1024], P('stage', 'data')
- grad_up: float32 [128, 1, 1024, 512], P(('stage', 'data'))
- mom_up: float32 [1, 1024, 512], P('stage', 'data')
- master_up: float32 [1, 1024, 512], P('stage', 'data')
- grad_down: float32 [128, 1, 512, 1024], P(('stage', 'data'))
- mom_down: float32 [1, 512, 1024], P('stage', 'data')
- master_down: float32 [1, 512, 1024], P('stage', 'data')
Outputs:
- output 1: float32 [1, 1024, 1024], P('stage', 'data')
- output 2: float32 [1, 1024, 1024], P('stage', 'data')
- output 3: bfloat16 [1, 1024, 1024], P('stage', 'data')
- output 4: float32 [1, 1024, 512], P('stage', 'data')
- output 5: float32 [1, 1024, 512], P('stage', 'data')
- output 6: bfloat16 [1, 1024, 512], P('stage', 'data')
- output 7: float32 [1, 512, 1024], P('stage', 'data')
- output 8: float32 [1, 512, 1024], P('stage', 'data')
- output 9: bfloat16 [1, 512, 1024], P('stage', 'data')
All inputs are finite; a program needn't handle non-finite values.
Results may differ from a plain program's by a relative error of at most 0.00763485.
Values are sent between devices in bfloat16 or wider.
A program may use at most 1 GiB of HBM per device.

v0:
```python
import math
import functools
import jax
import jax.numpy as jnp
from jax import lax
from jax.sharding import PartitionSpec as P, NamedSharding

MOMENTUM = 0.95
LEARN_RATE = 0.25
WEIGHT_DECAY = 0.2
EPSILON = 1e-7
COEF_A = 3.4445
COEF_B = -4.7750
COEF_C = 2.0315
NS_STEPS = 5


def newton_schulz(x_mat, is_tall):
    for _ in range(NS_STEPS):
        if is_tall:
            gram_mat = jnp.einsum('bkr,bkc->brc', x_mat, x_mat, preferred_element_type=jnp.float32)
        else:
            gram_mat = jnp.einsum('brk,bck->brc', x_mat, x_mat, preferred_element_type=jnp.float32)
        gram_mat = gram_mat.astype(jnp.bfloat16)
        gram_sq = jnp.einsum('brk,bkc->brc', gram_mat, gram_mat, preferred_element_type=jnp.float32).astype(jnp.bfloat16)
        poly_mat = (COEF_B * gram_mat.astype(jnp.float32) + COEF_C * gram_sq.astype(jnp.float32)).astype(jnp.bfloat16)
        if is_tall:
            update = jnp.einsum('bkc,brc->bkr', x_mat, poly_mat, preferred_element_type=jnp.float32)
        else:
            update = jnp.einsum('brc,bck->brk', poly_mat, x_mat, preferred_element_type=jnp.float32)
        x_mat = (COEF_A * x_mat.astype(jnp.float32) + update.astype(jnp.bfloat16).astype(jnp.float32)).astype(jnp.bfloat16)
    return x_mat


def stack_step(grad_all, mom_old, master_old, offset, group_size):
    count, rows_local, n_cols = mom_old.shape
    n_rows = rows_local * group_size
    grad_rows = lax.psum_scatter(grad_all[0], 'data', scatter_dimension=1, tiled=True) / group_size
    mom_new = MOMENTUM * mom_old + grad_rows
    norm_sq = lax.psum(jnp.sum(mom_new * mom_new, axis=(1, 2)), 'data')
    x_rows = (mom_new / (jnp.sqrt(norm_sq)[:, None, None] + EPSILON)).astype(jnp.bfloat16)
    slots = (count + offset + group_size - 1) // group_size
    padded = jnp.pad(x_rows, ((offset, slots * group_size - count - offset), (0, 0), (0, 0)))
    send_buf = padded.reshape(slots, group_size, rows_local, n_cols)
    owned = lax.all_to_all(send_buf, 'data', 1, 2, tiled=True).reshape(slots, n_rows, n_cols)
    positions = jnp.arange(slots) * group_size + lax.axis_index('data')
    has_work = jnp.any((positions >= offset) & (positions < offset + count))
    ortho_mat = lax.cond(has_work, functools.partial(newton_schulz, is_tall=n_rows > n_cols), jnp.zeros_like, owned)
    returned = lax.all_to_all(ortho_mat.reshape(slots, 1, n_rows, n_cols), 'data', 2, 1, tiled=True)
    ortho_rows = returned.reshape(slots * group_size, rows_local, n_cols)[offset:offset + count]
    scale = 0.2 * math.sqrt(max(n_rows, n_cols))
    master_new = master_old - LEARN_RATE * (scale * ortho_rows.astype(jnp.float32) + WEIGHT_DECAY * master_old)
    return [mom_new, master_new, master_new.astype(jnp.bfloat16)]


def solution(mesh):
    group_size = mesh.shape['data']
    grad_spec = P(('stage', 'data'), None, None, None)
    row_spec = P('stage', 'data', None)

    def step_local(*arrays):
        attn_count = arrays[1].shape[0]
        expert_count = arrays[4].shape[0]
        offsets = (0, attn_count % group_size, (attn_count + expert_count) % group_size)
        results = []
        for stack_idx in range(3):
            results.extend(stack_step(arrays[3 * stack_idx], arrays[3 * stack_idx + 1], arrays[3 * stack_idx + 2], offsets[stack_idx], group_size))
        return tuple(results)

    in_specs = (grad_spec, row_spec, row_spec) * 3
    out_specs = (row_spec,) * 9
    return jax.shard_map(step_local, mesh=mesh, in_specs=in_specs, out_specs=out_specs, check_vma=False)
```

profile of v0, /device:TPU:1, one launch (start us, length us, event | category | flops | bytes accessed | tf_op | source)
XLA Modules:
  0.0 1804.5 jit_solution(11361713226568852920)
XLA Ops:
  9.4 158.6 %all-reduce.7.cloned.1.call-done = f32[1,512,1024]{2,1,0:T(8,128)} async-done(((f32[1,512,1024]{2,1,0:T(8,128)}), f32[1,512,1024]{2,1,0:T(8,128)}) %all-reduce.7.cloned.1.call-update) | async-done | bytes 2097168
  168.0 1.4 multiply_reduce_fusion.1
  169.4 640.5 %reduce-scatter.6.cloned.1.call-done = f32[1,8,512]{2,1,0:T(8,128)} async-done(((f32[1,1024,512]{2,1,0:T(8,128)}), f32[1,8,512]{2,1,0:T(8,128)}) %reduce-scatter.6.cloned.1.call-update) | async-done | bytes 16400 | tf_op jit(solution)/shard_map/reduce_scatter | solution.py:38
  810.0 1.3 multiply_reduce_fusion.2
  811.3 644.4 %reduce-scatter.4.cloned.1.call-done = f32[1,8,1024]{2,1,0:T(8,128)} async-done(((f32[1,1024,1024]{2,1,0:T(8,128)}), f32[1,8,1024]{2,1,0:T(8,128)}) %reduce-scatter.4.cloned.1.call-update) | async-done | bytes 32784 | tf_op jit(solution)/shard_map/reduce_scatter | solution.py:38
  1455.7 1.4 multiply_reduce_fusion
  1457.1 69.2 %all-reduce.4 = (f32[1]{0:T(128)}, f32[1]{0:T(128)}, f32[1]{0:T(128)}) all-reduce(f32[1]{0:T(128)} %bitcast.14, f32[1]{0:T(128)} %bitcast.20, f32[1]{0:T(128)} %bitcast.26), channel_id=1, replica_groups=mesh['stage'=1,'data'=128] {'data'}, use_global_device_ids=true, to_apply=%region_2.0 | all-reduce | flops 3 | bytes 24 | tf_op jit(solution)/shard_map/psum | solution.py:40
  1527.0 1.3 pad_bitcast_fusion.1
  1528.3 4.7 all-to-all-start.4
  1534.7 17.3 all-to-all-done.4
  1552.0 4.4 all-to-all-start.2
  1557.1 1.6 pad_bitcast_fusion
  1558.7 16.8 all-to-all-done.2
  1575.6 5.5 all-to-all-start
  1581.4 1.6 copy.75
  1583.5 6.8 reduce.7
  1590.3 1.5 reshape.609
  1591.8 20.0 %all-to-all-done = bf16[1,128,8,1024]{3,2,0,1:T(8,128)(2,1)} async-done(((bf16[1,128,8,1024]{3,2,0,1:T(8,128)(2,1)}), bf16[1,128,8,1024]{3,2,0,1:T(8,128)(2,1)}, u32[]{:S(2)}, u32[]{:S(2)}) %all-to-all-start) | async-done | bytes 2097184 | tf_op jit(solution)/shard_map/all_to_all | solution.py:45
  1611.8 5.3 all-to-all-start.5
  1617.2 24.1 %conditional.4 = (bf16[1,1024,512]{1,2,0:T(8,128)(2,1)S(1)}) conditional(s32[]{:T(128)} %convert_element_type.629, () %tuple.27, bf16[1,128,8,512]{3,2,0,1:T(8,128)(2,1)S(1)} %copy-done.2), branch_computations={%region_8.9_spmd, %region_9.10_spmd} | conditional | flops 6737100800 | bytes 28311588 | solution.py:48
  1618.2 1.6 fusion.71
  1619.7 3.4 fusion.49
  1623.1 3.2 convolution_convert_fusion.17
  1626.3 2.4 add_convert_fusion.28
  1628.7 1.5 convolution_convert_fusion.16
  1630.3 2.6 add_convert_fusion.27
  1632.9 1.5 convolution_convert_fusion.15
  1634.4 2.6 add_convert_fusion.26
  1637.0 1.5 convolution_convert_fusion.14
  1638.6 2.6 fusion.50
  1642.3 4.6 copy.53
  1646.9 8.0 reduce.6
  1655.0 2.3 reshape.607
  1657.2 4.7 all-to-all-start.3
  1661.9 5.3 conditional.3
  1667.3 5.2 copy.74
  1672.5 12.8 reduce.5
  1685.2 2.6 reshape.605
  1687.9 68.4 %all-to-all-start.1 = ((bf16[128,2,4096]{2,1,0:T(2,128)(2,1)}), bf16[128,2,4096]{2,1,0:T(2,128)(2,1)S(1)}, u32[]{:S(2)}, u32[]{:S(2)}) async-start(bf16[128,2,4096]{2,1,0:T(2,128)(2,1)} %reshape.605), calls=%async_computation.2 | async-start | bytes 4194304 | tf_op jit(solution)/shard_map/all_to_all | solution.py:49
  1756.2 3.4 reshape.610
  1759.7 7.8 bitcast_reduce_fusion
  1767.4 1.2 all_to_all.29
  1768.7 7.5 reshape.608
  1776.1 1.9 copy.73
  1778.0 1.3 fusion.158
  1780.0 7.1 all-to-all-done.1
  1787.1 6.7 reshape.606
  1793.8 3.0 copy.72
  (45 shorter events, 7.2 us)
Async XLA Ops:
  7.2 160.9 %all-reduce.7.cloned.1.call-start = ((), (), s32[]{:S(2)}) async-start(), calls=%async_computation.10 | async-start | bytes 4194304
  7.9 802.0 %reduce-scatter.6.cloned.1.call-start = ((), (), s32[]{:S(2)}) async-start(), calls=%async_computation.9 | async-start | bytes 2113536 | tf_op jit(solution)/shard_map/reduce_scatter | solution.py:38
  8.7 1447.0 %reduce-scatter.4.cloned.1.call-start = ((), (), s32[]{:S(2)}) async-start(), calls=%async_computation.8 | async-start | bytes 4227072 | tf_op jit(solution)/shard_map/reduce_scatter | solution.py:38
  8.7 159.3 %copy-start.8 = (f32[1,4,1024]{2,1,0:T(4,128)S(1)}, f32[1,4,1024]{2,1,0:T(4,128)}, u32[]{:S(2)}) copy-start(f32[1,4,1024]{2,1,0:T(4,128)} %param.22) | copy-start | bytes 49156
  8.7 801.2 %copy-start.9 = (f32[1,8,512]{2,1,0:T(8,128)S(1)}, f32[1,8,512]{2,1,0:T(8,128)}, u32[]{:S(2)}) copy-start(f32[1,8,512]{2,1,0:T(8,128)} %param.19) | copy-start | bytes 49156
  8.7 1447.0 %copy-start.6 = (f32[1,8,1024]{2,1,0:T(8,128)S(1)}, f32[1,8,1024]{2,1,0:T(8,128)}, u32[]{:S(2)}) copy-start(f32[1,8,1024]{2,1,0:T(8,128)} %param.16) | copy-start | bytes 98308
  169.4 1365.3 %copy-start.4 = (f32[1,4,1024]{2,1,0:T(4,128)}, f32[1,4,1024]{2,1,0:T(4,128)S(1)}, u32[]{:S(2)}) copy-start(f32[1,4,1024]{2,1,0:T(4,128)S(1)} %get-tuple-element.34) | copy-start | bytes 49156
  811.3 723.4 %copy-start.5 = (f32[1,8,512]{2,1,0:T(8,128)}, f32[1,8,512]{2,1,0:T(8,128)S(1)}, u32[]{:S(2)}) copy-start(f32[1,8,512]{2,1,0:T(8,128)S(1)} %get-tuple-element.36) | copy-start | bytes 49156
  1457.1 100.1 %copy-start.3 = (f32[1,8,1024]{2,1,0:T(8,128)}, f32[1,8,1024]{2,1,0:T(8,128)S(1)}, u32[]{:S(2)}) copy-start(f32[1,8,1024]{2,1,0:T(8,128)S(1)} %get-tuple-element.38) | copy-start | bytes 98308
  1528.3 23.7 %all-to-all-start.4 = ((bf16[1,128,4,1024]{3,2,0,1:T(4,128)(2,1)}), bf16[1,128,4,1024]{3,2,0,1:T(4,128)(2,1)S(1)}, u32[]{:S(2)}, u32[]{:S(2)}) async-start(bf16[1,128,4,1024]{3,2,0,1:T(4,128)(2,1)} %pad_bitcast_fusion.1), calls=%async_computation.6 | async-start | bytes 2097152 | tf_op jit(solution)/shard_map/all_to_all | solution.py:45
  1552.0 23.6 %all-to-all-start.2 = ((bf16[1,128,8,512]{3,2,0,1:T(8,128)(2,1)}), bf16[1,128,8,512]{3,2,0,1:T(8,128)(2,1)S(1)}, u32[]{:S(2)}, u32[]{:S(2)}) async-start(bf16[1,128,8,512]{3,2,0,1:T(8,128)(2,1)} %pad_bitcast_fusion.2), calls=%async_computation.4 | async-start | bytes 2097152 | tf_op jit(solution)/shard_map/all_to_all | solution.py:45
  1575.6 5.5 copy-start.1
  1575.6 36.3 %all-to-all-start = ((bf16[1,128,8,1024]{3,2,0,1:T(8,128)(2,1)}), bf16[1,128,8,1024]{3,2,0,1:T(8,128)(2,1)}, u32[]{:S(2)}, u32[]{:S(2)}) async-start(bf16[1,128,8,1024]{3,2,0,1:T(8,128)(2,1)} %pad_bitcast_fusion), calls=%async_computation.1 | async-start | bytes 4194304 | tf_op jit(solution)/shard_map/all_to_all | solution.py:45
  1590.3 26.9 %copy-start.2 = (bf16[1,128,8,512]{3,2,0,1:T(8,128)(2,1)S(1)}, bf16[1,128,8,512]{3,2,0,1:T(8,128)(2,1)}, u32[]{:S(2)}) copy-start(bf16[1,128,8,512]{3,2,0,1:T(8,128)(2,1)} %copy-done.1) | copy-start | bytes 3145732
  1611.8 45.4 %all-to-all-start.5 = ((bf16[128,2,2048]{2,1,0:T(2,128)(2,1)}), bf16[128,2,2048]{2,1,0:T(2,128)(2,1)S(1)}, u32[]{:S(2)}, u32[]{:S(2)}) async-start(bf16[128,2,2048]{2,1,0:T(2,128)(2,1)} %reshape.609), calls=%async_computation.7 | async-start | bytes 2097152 | tf_op jit(solution)/shard_map/all_to_all | solution.py:49
  1623.1 3.2 copy-start.12
  1641.3 1.0 copy-start
  1657.2 30.6 %all-to-all-start.3 = ((bf16[128,2,2048]{2,1,0:T(2,128)(2,1)}), bf16[128,2,2048]{2,1,0:T(2,128)(2,1)}, u32[]{:S(2)}, u32[]{:S(2)}) async-start(bf16[128,2,2048]{2,1,0:T(2,128)(2,1)} %reshape.607), calls=%async_computation.5 | async-start | bytes 2097152 | tf_op jit(solution)/shard_map/all_to_all | solution.py:49
  1687.9 99.2 %all-to-all-start.1 = ((bf16[128,2,4096]{2,1,0:T(2,128)(2,1)}), bf16[128,2,4096]{2,1,0:T(2,128)(2,1)S(1)}, u32[]{:S(2)}, u32[]{:S(2)}) async-start(bf16[128,2,4096]{2,1,0:T(2,128)(2,1)} %reshape.605), calls=%async_computation.2 | async-start | bytes 4194304 | tf_op jit(solution)/shard_map/all_to_all | solution.py:49
  1776.1 1.9 copy-start.10
  1776.1 3.2 copy-start.11
  1793.8 3.0 copy-start.7
Sparse Core Ops, SparseCore 0:
  12.8 155.1 all-reduce.6
  170.4 639.5 reduce-scatter.5
  812.3 643.3 reduce-scatter.3
where the time goes:
time: 1810 us; the launch traced here: 1800 us
  waiting for transfers between devices  1510 us (83%)
  starting transfers between devices  93.1 us (5%)
  blocking collectives  69.2 us (4%)
  local copies, waits for them, and re-layouts  55.7 us (3%)
  other arithmetic  34.2 us (2%)
  matrix products  23 us (1%)
    reduce_scatter x2, waiting for transfers between devices, stack_step(): lax.psum_scatter(grad_all[0], 'data', scatter_dimension=1, tiled=True)  1280 us
    unnamed x4, waiting for transfers between devices  161 us
    all_to_all x3, starting transfers between devices, stack_step(): lax.all_to_all(ortho_mat.reshape(slots, 1, n_rows, n_cols), 'data', 2, 1,...  78.4 us
    psum x1, blocking collectives, stack_step(): norm_sq = lax.psum(jnp.sum(mom_new * mom_new, axis=(1, 2)), 'data')  69.2 us
    all_to_all x3, waiting for transfers between devices, stack_step(): lax.all_to_all(send_buf, 'data', 1, 2, tiled=True)  54.1 us
  transfers between devices with their start and end apart: 9, of which 7 were waited for; matrix products, arithmetic and copies ran while one was open for 5% of the time, Pallas kernels for 0%

commit v1 on v0

v1 whole, which is shorter than its diff:
```python
import functools
import math

import jax
import jax.numpy as jnp
from jax import lax
from jax.experimental import pallas as pl
from jax.experimental.pallas import tpu as pltpu
from jax.sharding import PartitionSpec as P

MOMENTUM = 0.95
LEARN_RATE = 0.25
WEIGHT_DECAY = 0.2
EPSILON = 1e-7
COEF_A = 3.4445
COEF_B = -4.7750
COEF_C = 2.0315
NS_STEPS = 5

F32 = jnp.float32
BF16 = jnp.bfloat16

COLS = ((0, 384), (384, 384), (768, 256))
ORDER = ((0, 1, 2), (1, 2, 0), (2, 0, 1))
SIDE = 4
CHIP_ROWS = 16
WIDE = 1024
NARROW = 512
TILE = 256
BLOCK = (SIDE, SIDE, SIDE, CHIP_ROWS, WIDE)
ALL = slice(None)
LO = pl.ds(0, 8)
HI = pl.ds(8, 8)
HALF = (LO, HI)
WEST = pl.ds(0, NARROW)
EAST = pl.ds(NARROW, NARROW)
PIECES = (
    (('up', 0, 384, ALL, 0),),
    (('up', 384, 128, ALL, 384), ('down', 0, TILE, LO, NARROW), ('down', NARROW, TILE, HI, NARROW)),
    (('down', TILE, TILE, LO, 768), ('down', 768, TILE, HI, 768)),
)


def place(ref, fixed, rows, cols):
    return ref.at[region(fixed, rows, cols)]


def region(fixed, rows, cols):
    return tuple(fixed.get(axis, ALL) for axis in range(3)) + (rows, cols)


def coords_of(k):
    return k // (SIDE * SIDE), lax.rem(k // SIDE, SIDE), lax.rem(k, SIDE)


def aligned(start, size):
    return pl.ds(pl.multiple_of(start, size), size)


def kernel(group_size, grad_attn, grad_up, grad_down, mom_attn, mom_up, mom_down, mas_attn, mas_up, mas_down,
           mo_attn, wo_attn, bo_attn, mo_up, wo_up, bo_up, mo_down, wo_down, bo_down,
           own, peer, full, recv0, recv1, recv2, mom_pk, swap_attn, swap_up, swap_down,
           send_attn, send_up, send_down, got_attn, got_up, got_down, x_mat, a_mat, b_mat, turn,
           load_sem, push_sem, pull_sem, rs_send, rs_recv, ag_send, ag_recv, ex_send, ex_recv):
    me = lax.axis_index('data')
    core = lax.rem(me, 2)
    chip = me // 2
    pos = coords_of(chip)
    partner = me + 1 - 2 * core
    recvs = (recv0, recv1, recv2)

    def at_axis(axis, coord):
        coords = list(pos)
        coords[axis] = coord
        return ((coords[0] * SIDE + coords[1]) * SIDE + coords[2]) * 2 + core

    right = [lax.rem(p + 1, SIDE) for p in pos]
    left = [lax.rem(p + 3, SIDE) for p in pos]
    far = [lax.rem(p + 2, SIDE) for p in pos]
    right_dev = [at_axis(a, right[a]) for a in range(3)]
    left_dev = [at_axis(a, left[a]) for a in range(3)]

    def remote(src, dst, send_sem, recv_sem, device):
        return pltpu.make_async_remote_copy(src_ref=src, dst_ref=dst, send_sem=send_sem, recv_sem=recv_sem,
                                            device_id={'data': device}, device_id_type=pl.DeviceIdType.MESH)

    barrier = pltpu.get_barrier_semaphore()
    for device in [partner] + right_dev + left_dev:
        pl.semaphore_signal(barrier, inc=1, device_id={'data': device}, device_id_type=pl.DeviceIdType.MESH)
    pl.semaphore_wait(barrier, 7)

    def turns(color):
        axis = ORDER[color][0]
        return axis, (far[axis], right[axis], left[axis], pos[axis])

    def attn_copy(color, turn_idx, push):
        axis, coords = turns(color)
        cols = pl.ds(*COLS[color])
        src = place(grad_attn, {axis: coords[turn_idx]}, ALL, cols)
        if push:
            dst = place(peer, {axis: coords[turn_idx]}, ALL, cols)
            return remote(src, dst, push_sem.at[color, turn_idx, 0], pull_sem.at[color, turn_idx, 0], partner)
        dst = place(own, {axis: coords[turn_idx]}, ALL, cols)
        return pltpu.make_async_copy(src, dst, load_sem.at[color, turn_idx, 0])

    def expert_copies(color, turn_idx, push):
        axis, coords = turns(color)
        copies = []
        for k, (source, col, width, rows, packed) in enumerate(PIECES[color]):
            src = place(grad_up if source == 'up' else grad_down, {axis: coords[turn_idx]}, ALL, pl.ds(col, width))
            target = peer if push else own
            dst = place(target, {axis: coords[turn_idx]}, rows, pl.ds(packed, width))
            if push:
                copies.append(remote(src, dst, push_sem.at[color, turn_idx, k], pull_sem.at[color, turn_idx, k], partner))
            else:
                copies.append(pltpu.make_async_copy(src, dst, load_sem.at[color, turn_idx, k]))
        return copies

    def mom_copies_from_0():
        return [remote(mom_up, swap_up, ex_send.at[0], ex_recv.at[0], partner),
                remote(mom_down, swap_down, ex_send.at[1], ex_recv.at[1], partner)]

    def mom_copies_from_1():
        return [remote(mom_attn, swap_attn, ex_send.at[0], ex_recv.at[0], partner)]

    @pl.when(core == 0)
    def _():
        for turn_idx in range(SIDE):
            for color in range(3):
                attn_copy(color, turn_idx, False).start()
                for copy in expert_copies(color, turn_idx, True):
                    copy.start()
        for copy in mom_copies_from_0():
            copy.start()

    @pl.when(core == 1)
    def _():
        for turn_idx in range(SIDE):
            for color in range(3):
                for copy in expert_copies(color, turn_idx, False):
                    copy.start()
                attn_copy(color, turn_idx, True).start()
        for copy in mom_copies_from_1():
            copy.start()

    def chip_sum(color, turn_idx):
        @pl.when(core == 0)
        def _():
            attn_copy(color, turn_idx, False).wait()
            attn_copy(color, turn_idx, True).wait_recv()

        @pl.when(core == 1)
        def _():
            for copy in expert_copies(color, turn_idx, False):
                copy.wait()
            for copy in expert_copies(color, turn_idx, True):
                copy.wait_recv()
        axis, coords = turns(color)
        idx = region({axis: coords[turn_idx]}, ALL, pl.ds(*COLS[color]))
        own[idx] = own[idx] + peer[idx]

    def rs_ctx(phase, color):
        order = ORDER[color]
        axis = order[phase]
        fixed = {order[k]: pos[order[k]] for k in range(phase)}
        return axis, fixed, pl.ds(*COLS[color])

    def rs_buf(phase, color, piece):
        col, width = COLS[color]
        lead = (piece,) + (ALL,) * (2 - phase)
        return recvs[phase].at[lead + (ALL, pl.ds(col, width))]

    def rs_copy(phase, color, piece):
        axis, fixed, cols = rs_ctx(phase, color)
        coord, half, device = ((far, 0, right_dev), (far, 1, left_dev), (right, 1, right_dev),
                               (left, 0, left_dev), (right, 0, right_dev), (left, 1, left_dev))[piece]
        src = place(own, {**fixed, axis: coord[axis]}, HALF[half], cols)
        return remote(src, rs_buf(phase, color, piece), rs_send.at[phase, color, piece], rs_recv.at[phase, color, piece],
                      device[axis])

    def rs_add(phase, color, coord, half, pieces):
        axis, fixed, cols = rs_ctx(phase, color)
        idx = region({**fixed, axis: coord[axis]}, HALF[half], cols)
        total = own[idx]
        for piece in pieces:
            col, width = COLS[color]
            lead = (piece,) + (ALL,) * (2 - phase)
            total = total + recvs[phase][lead + (ALL, pl.ds(col, width))]
        own[idx] = total

    def rs_mid(phase, color):
        rs_copy(phase, color, 0).wait_recv()
        rs_add(phase, color, right, 0, (0,))
        rs_copy(phase, color, 4).start()
        rs_copy(phase, color, 1).wait_recv()
        rs_add(phase, color, left, 1, (1,))
        rs_copy(phase, color, 5).start()

    def rs_end(phase, color):
        for piece in (2, 3, 4, 5):
            rs_copy(phase, color, piece).wait_recv()
        rs_add(phase, color, pos, 0, (3, 4))
        rs_add(phase, color, pos, 1, (2, 5))

    for color in range(3):
        chip_sum(color, 0)
        rs_copy(0, color, 0).start()
        rs_copy(0, color, 1).start()
    for color in range(3):
        chip_sum(color, 1)
        rs_copy(0, color, 2).start()
    for color in range(3):
        chip_sum(color, 2)
        rs_copy(0, color, 3).start()
    for color in range(3):
        rs_mid(0, color)
    for color in range(3):
        chip_sum(color, 3)
    for phase in range(3):
        if phase > 0:
            for color in range(3):
                rs_mid(phase, color)
        for color in range(3):
            rs_end(phase, color)
            if phase < 2:
                for piece in range(4):
                    rs_copy(phase + 1, color, piece).start()

    @pl.when(core == 0)
    def _():
        mom_copies_from_1()[0].wait_recv()
        mom_pk[LO] = mom_attn[...]
        mom_pk[HI] = swap_attn[...]

    @pl.when(core == 1)
    def _():
        for copy in mom_copies_from_0():
            copy.wait_recv()
        mom_pk[LO, WEST] = swap_up[...]
        mom_pk[HI, WEST] = mom_up[...]
        for first, cols in ((0, WEST), (8, EAST)):
            mom_pk[pl.ds(first, SIDE), EAST] = swap_down[:, cols]
            mom_pk[pl.ds(first + SIDE, SIDE), EAST] = mom_down[:, cols]

    mine = pos
    mom_new = MOMENTUM * mom_pk[...] + own[mine] * (1.0 / group_size)
    full[mine] = mom_new

    def ag_copy(phase, color, piece):
        order = ORDER[color]
        axis = order[phase]
        fixed = {order[k]: pos[order[k]] for k in range(phase)}
        coord, half, device = ((pos, 0, right_dev), (pos, 1, left_dev), (pos, 1, right_dev), (pos, 0, left_dev),
                               (left, 0, right_dev), (right, 1, left_dev))[piece]
        part = place(full, {**fixed, axis: coord[axis]}, HALF[half], pl.ds(*COLS[color]))
        return remote(part, part, ag_send.at[phase, color, piece], ag_recv.at[phase, color, piece], device[axis])

    def ag_arrive(phase, color, piece):
        order = ORDER[color]
        axis = order[phase]
        fixed = {order[k]: pos[order[k]] for k in range(phase)}
        coord, half = ((left, 0), (right, 1), (left, 1), (right, 0), (far, 0), (far, 1))[piece]
        part = place(full, {**fixed, axis: coord[axis]}, HALF[half], pl.ds(*COLS[color]))
        remote(part, part, ag_send.at[phase, color, piece], ag_recv.at[phase, color, piece], right_dev[axis]).wait_recv()

    for color in range(3):
        for piece in range(4):
            ag_copy(2, color, piece).start()
    for phase in (2, 1, 0):
        for color in range(3):
            ag_arrive(phase, color, 0)
            ag_copy(phase, color, 4).start()
            ag_arrive(phase, color, 1)
            ag_copy(phase, color, 5).start()
        for color in range(3):
            for piece in (2, 3, 4, 5):
                ag_arrive(phase, color, piece)
            if phase > 0:
                for piece in range(4):
                    ag_copy(phase - 1, color, piece).start()

    @pl.when(core == 0)
    def _():
        send_attn[...] = full[mine + (HI, ALL)]
        mo_attn[...] = full[mine + (LO, ALL)]

    @pl.when(core == 1)
    def _():
        send_up[...] = full[mine + (LO, WEST)]
        mo_up[...] = full[mine + (HI, WEST)]
        for rows, cols in ((LO, WEST), (HI, EAST)):
            down = full[mine + (rows, EAST)]
            send_down[:, cols] = down[:SIDE]
            mo_down[:, cols] = down[SIDE:]

    def back_from_0(base, out_attn):
        return [remote(send_attn, out_attn, ex_send.at[base], ex_recv.at[base], partner)]

    def back_from_1(base, out_up, out_down):
        return [remote(send_up, out_up, ex_send.at[base], ex_recv.at[base], partner),
                remote(send_down, out_down, ex_send.at[base + 1], ex_recv.at[base + 1], partner)]

    @pl.when(core == 0)
    def _():
        for copy in back_from_0(2, mo_attn):
            copy.start()

    @pl.when(core == 1)
    def _():
        for copy in back_from_1(2, mo_up, mo_down):
            copy.start()

    def weighted(a_val, q_val):
        return (COEF_B * a_val.astype(F32) + COEF_C * q_val.astype(BF16).astype(F32)).astype(BF16)

    def advance(x_val, y_val):
        return (COEF_A * x_val.astype(F32) + y_val.astype(BF16).astype(F32)).astype(BF16)

    def gram(base, size):
        rows = pl.ds(base, size)

        def body(j, carry):
            off = pl.multiple_of(j * TILE, TILE)
            a_val = lax.dot_general(x_mat[rows, :], x_mat[aligned(base + off, TILE), :], (((1,), (1,)), ((), ())),
                                    preferred_element_type=F32)
            a_mat[rows, pl.ds(off, TILE)] = a_val.astype(BF16)
            return carry
        lax.fori_loop(0, size // TILE, body, 0)

    def poly(base, size):
        rows = pl.ds(base, size)

        def body(j, carry):
            cols = aligned(j * TILE, TILE)
            q_val = jnp.dot(a_mat[rows, 0:size], a_mat[rows, cols], preferred_element_type=F32)
            b_mat[rows, cols] = weighted(a_mat[rows, cols], q_val)
            return carry
        lax.fori_loop(0, size // TILE, body, 0)

    def update(base, size):
        rows = pl.ds(base, size)

        def body(j, carry):
            cols = aligned(j * TILE, TILE)
            y_val = jnp.dot(b_mat[rows, 0:size], x_mat[rows, cols], preferred_element_type=F32)
            x_mat[rows, cols] = advance(x_mat[rows, cols], y_val)
            return carry
        lax.fori_loop(0, 4, body, 0)

    def square_sum(cols):
        def body(k, acc):
            val = full[coords_of(k) + (ALL, cols)]
            return acc + val * val
        acc = lax.fori_loop(0, 64, body, jnp.zeros((16, cols.size), F32))
        return jnp.sum(acc, axis=(0, 1), keepdims=True)

    def inverse(total):
        return 1.0 / (jnp.sqrt(total) + EPSILON)

    @pl.when(core == 0)
    def _():
        scale = inverse(square_sum(pl.ds(0, WIDE)))

        def fill(k, carry):
            val = full[coords_of(k)]
            x_mat[aligned(k * CHIP_ROWS, CHIP_ROWS), :] = (val * scale).astype(BF16)
            return carry
        lax.fori_loop(0, 64, fill, 0)

        def step(_, carry):
            gram(0, WIDE)
            poly(0, WIDE)
            update(0, WIDE)
            return carry
        lax.fori_loop(0, NS_STEPS - 1, step, 0)
        gram(0, WIDE)
        rows = aligned(chip * CHIP_ROWS, CHIP_ROWS)
        a_val = a_mat[rows, :]
        b_val = weighted(a_val, jnp.dot(a_val, a_mat[...], preferred_element_type=F32))
        out = advance(x_mat[rows, :], jnp.dot(b_val, x_mat[...], preferred_element_type=F32)).astype(F32)
        back_from_0(2, mo_attn)[0].wait_send()
        send_attn[...] = out[8:]
        got_attn[...] = out[:8]
        back_from_0(4, got_attn)[0].start()

    @pl.when(core == 1)
    def _():
        scale_up = inverse(square_sum(WEST))
        scale_down = inverse(square_sum(EAST))

        def fill_up(k, carry):
            val = full[k // 2, pl.ds(2 * lax.rem(k, 2), 2), :, :, WEST].reshape(128, NARROW)
            x_mat[WEST, aligned(k * 128, 128)] = jnp.transpose(val * scale_up).astype(BF16)
            return carry
        lax.fori_loop(0, 8, fill_up, 0)

        def fill_down(k, carry):
            z, y, x = coords_of(2 * k)
            val = full[z, y, pl.ds(x, 2), :, EAST] * scale_down
            rows = aligned(NARROW + k * CHIP_ROWS, CHIP_ROWS)
            x_mat[rows, WEST] = val[:, :8].reshape(CHIP_ROWS, NARROW).astype(BF16)
            x_mat[rows, EAST] = val[:, 8:].reshape(CHIP_ROWS, NARROW).astype(BF16)
            return carry
        lax.fori_loop(0, 32, fill_down, 0)

        def matrix(t, carry):
            base = pl.multiple_of(t * NARROW, NARROW)

            def step(_, carry):
                gram(base, NARROW)
                poly(base, NARROW)
                update(base, NARROW)
                return carry
            lax.fori_loop(0, NS_STEPS - 1, step, 0)
            gram(base, NARROW)
            return carry
        lax.fori_loop(0, 2, matrix, 0)
        poly(0, NARROW)
        cols = aligned(chip // 8 * 128, 128)
        out_up = advance(x_mat[WEST, cols], jnp.dot(b_mat[WEST, WEST], x_mat[WEST, cols], preferred_element_type=F32))
        turn[...] = jnp.transpose(out_up.astype(F32))
        rows = aligned(NARROW + chip // 2 * CHIP_ROWS, CHIP_ROWS)
        a_val = a_mat[rows, WEST]
        b_val = weighted(a_val, jnp.dot(a_val, a_mat[EAST, WEST], preferred_element_type=F32))
        both = advance(x_mat[rows, :], jnp.dot(b_val, x_mat[EAST, :], preferred_element_type=F32)).astype(F32)
        out_down = jnp.where(lax.rem(chip, 2) == 0, both[:8], both[8:])
        for copy in back_from_1(2, mo_up, mo_down):
            copy.wait_send()
        first = pl.multiple_of(lax.rem(chip, 8) * CHIP_ROWS, CHIP_ROWS)
        send_up[...] = turn[pl.ds(first, 8), :]
        got_up[...] = turn[pl.ds(first + 8, 8), :]
        send_down[...] = out_down[:SIDE]
        got_down[...] = out_down[SIDE:]
        for copy in back_from_1(4, got_up, got_down):
            copy.start()

    @pl.when(core == 0)
    def _():
        for copy in back_from_1(2, mo_up, mo_down) + back_from_1(4, got_up, got_down):
            copy.wait_recv()

    @pl.when(core == 1)
    def _():
        for copy in back_from_0(2, mo_attn) + back_from_0(4, got_attn):
            copy.wait_recv()

    for mas, got, w_out, b_out in ((mas_attn, got_attn, wo_attn, bo_attn), (mas_up, got_up, wo_up, bo_up),
                                   (mas_down, got_down, wo_down, bo_down)):
        old = mas[...]
        new = old - LEARN_RATE * (0.2 * math.sqrt(WIDE) * got[...] + WEIGHT_DECAY * old)
        w_out[...] = new
        b_out[...] = new.astype(BF16)

    @pl.when(core == 0)
    def _():
        for turn_idx in range(SIDE):
            for color in range(3):
                for copy in expert_copies(color, turn_idx, True):
                    copy.wait_send()
        for copy in mom_copies_from_0() + back_from_0(4, got_attn):
            copy.wait_send()

    @pl.when(core == 1)
    def _():
        for turn_idx in range(SIDE):
            for color in range(3):
                attn_copy(color, turn_idx, True).wait_send()
        for copy in mom_copies_from_1() + back_from_1(4, got_up, got_down):
            copy.wait_send()

    for phase in range(3):
        for color in range(3):
            for piece in range(6):
                rs_copy(phase, color, piece).wait_send()
                ag_copy(phase, color, piece).wait_send()


def solution(mesh):
    group_size = mesh.shape['data']
    grad_spec = P(('stage', 'data'), None, None, None)
    row_spec = P('stage', 'data', None)

    def step_local(grad_attn, mom_attn, mas_attn, grad_up, mom_up, mas_up, grad_down, mom_down, mas_down):
        vmem = pl.BlockSpec(memory_space=pltpu.VMEM)
        hbm = pl.BlockSpec(memory_space=pl.ANY)
        shapes = ((8, WIDE), (8, NARROW), (SIDE, WIDE))
        outs = []
        for shape in shapes:
            outs += [jax.ShapeDtypeStruct(shape, F32), jax.ShapeDtypeStruct(shape, F32), jax.ShapeDtypeStruct(shape, BF16)]
        sem = pltpu.SemaphoreType.DMA
        scratch = [
            *[pltpu.VMEM(BLOCK, F32)] * 3,
            *[pltpu.VMEM((6,) + (SIDE,) * free + (8, WIDE), F32) for free in (2, 1, 0)],
            pltpu.VMEM((CHIP_ROWS, WIDE), F32),
            *[pltpu.VMEM(shape, F32) for shape in shapes * 3],
            *[pltpu.VMEM((WIDE, WIDE), BF16)] * 3,
            pltpu.VMEM((128, NARROW), F32),
            *[sem((3, SIDE, 3))] * 3,
            *[sem((3, 3, 6))] * 4,
            *[sem((6,))] * 2,
        ]
        result = pl.pallas_call(
            functools.partial(kernel, group_size),
            out_shape=outs,
            in_specs=[hbm] * 3 + [vmem] * 6,
            out_specs=[vmem] * 9,
            scratch_shapes=scratch,
            compiler_params=pltpu.CompilerParams(collective_id=0, has_side_effects=True, vmem_limit_bytes=60 * 1024 * 1024),
            name='muon',
        )(grad_attn.reshape(BLOCK), grad_up.reshape(BLOCK[:4] + (NARROW,)), grad_down.reshape(BLOCK[:3] + (8, WIDE)),
          *(v[0] for v in (mom_attn, mom_up, mom_down, mas_attn, mas_up, mas_down)))
        return tuple(r[None] for r in result)

    return jax.shard_map(step_local, mesh=mesh, in_specs=(grad_spec, row_spec, row_spec) * 3, out_specs=(row_spec,) * 9,
                         check_vma=False)
```

time: 1810 us -> 125 us (0.07)
  waiting for transfers between devices: 1510 us -> 0 us
  Pallas kernels: 0 us -> 111 us
  starting transfers between devices: 93.1 us -> 0 us
  blocking collectives: 69.2 us -> 0 us
  local copies, waits for them, and re-layouts: 55.7 us -> 12 us
  other arithmetic: 34.2 us -> 0 us
  matrix products: 23 us -> 0 us
    reduce_scatter x2 -> x0, waiting for transfers between devices: 1280 us -> none  [stack_step(): lax.psum_scatter(grad_all[0], 'data', scatter_dimension=1, tiled=True)]
    unnamed x4 -> x0, waiting for transfers between devices: 161 us -> none
    pallas_call x0 -> x1, Pallas kernels: none -> 111 us  [step_local(): pl.pallas_call(functools.partial(kernel, group_size), out_shape=outs, in_...]
    all_to_all x6 -> x0, starting transfers between devices: 93 us -> none  [the longest x3 78.4 us: stack_step(): lax.all_to_all(ortho_mat.reshape(slots, 1, n_rows, n_cols), 'data', 2, 1,...]
    psum x1 -> x0, blocking collectives: 69.2 us -> none  [stack_step(): norm_sq = lax.psum(jnp.sum(mom_new * mom_new, axis=(1, 2)), 'data')]
    all_to_all x6 -> x0, waiting for transfers between devices: 61.2 us -> none  [the longest x3 54.1 us: stack_step(): lax.all_to_all(send_buf, 'data', 1, 2, tiled=True)]
    unnamed x3 -> x0, other arithmetic: 27.6 us -> none
    dot_general x10 -> x0, matrix products: 23 us -> none  [the longest x5 13.6 us: newton_schulz(): jnp.einsum('bkc,brc->bkr', x_mat, poly_mat, preferred_element_type=jnp.fl...]
  transfers between devices with their start and end apart: 9 -> 0, of which waited for: 7 -> 0; matrix products, arithmetic and copies ran while one was open for 5% -> 0% of each run, Pallas kernels for 0% -> 0%
where the time goes in v1:
time: 125 us; the launch traced here: 124 us
  Pallas kernels  111 us (89%)
  local copies, waits for them, and re-layouts  12 us (10%)
    pallas_call x1, Pallas kernels, step_local(): pl.pallas_call(functools.partial(kernel, group_size), out_shape=outs, in_...  111 us
    unnamed x9, local copies, waits for them, and re-layouts  12 us

profile of v1, /device:TPU:1, one launch (start us, length us, event | category | flops | bytes accessed | tf_op | source)
XLA Modules:
  0.0 123.7 jit_solution(5383204694899806727)
XLA Ops:
  0.6 111.0 %muon.1 = (f32[8,1024]{1,0:T(8,128)}, f32[8,1024]{1,0:T(8,128)}, bf16[8,1024]{1,0:T(8,128)(2,1)}, f32[8,512]{1,0:T(8,128)}, f32[8,512]{1,0:T(8,128)}, /*index=5*...) custom-call(f32[4,4,4,16,1024]{4,3,2,1,0:T(8,128)} %bitcast.18, ...), custom_call_target="tpu_custom_call" | custom-call | tf_op jit(solution)/shard_map/muon/pallas_call | solution.py:502
  111.7 1.4 %copy.27 = f32[1,8,1024]{2,1,0:T(8,128)} copy(f32[1,8,1024]{2,1,0:T(8,128)} %bitcast.24) | data formatting | bytes 65536
  113.1 1.4 %copy.28 = f32[1,8,1024]{2,1,0:T(8,128)} copy(f32[1,8,1024]{2,1,0:T(8,128)} %bitcast.23) | data formatting | bytes 65536
  114.4 1.3 %copy.29 = bf16[1,8,1024]{2,1,0:T(8,128)(2,1)} copy(bf16[1,8,1024]{2,1,0:T(8,128)(2,1)} %bitcast.33) | data formatting | bytes 32768
  115.8 1.3 %copy.30 = f32[1,8,512]{2,1,0:T(8,128)} copy(f32[1,8,512]{2,1,0:T(8,128)} %bitcast.32) | data formatting | bytes 32768
  117.1 1.3 %copy.31 = f32[1,8,512]{2,1,0:T(8,128)} copy(f32[1,8,512]{2,1,0:T(8,128)} %bitcast.31) | data formatting | bytes 32768
  118.4 1.3 %copy.32 = bf16[1,8,512]{2,1,0:T(8,128)(2,1)} copy(bf16[1,8,512]{2,1,0:T(8,128)(2,1)} %bitcast.35) | data formatting | bytes 16384
  119.7 1.3 %copy.33 = f32[1,4,1024]{2,1,0:T(4,128)} copy(f32[1,4,1024]{2,1,0:T(4,128)} %bitcast.30) | data formatting | bytes 32768
  121.0 1.3 %copy.34 = f32[1,4,1024]{2,1,0:T(4,128)} copy(f32[1,4,1024]{2,1,0:T(4,128)} %bitcast.29) | data formatting | bytes 32768
  122.4 1.3 %copy.35 = bf16[1,4,1024]{2,1,0:T(4,128)(2,1)} copy(bf16[1,4,1024]{2,1,0:T(4,128)(2,1)} %bitcast.34) | data formatting | bytes 16384

commit v2 on v1

--- a/solution.py
+++ b/solution.py
@@ -57,10 +57,10 @@
     return pl.ds(pl.multiple_of(start, size), size)
 
 
-def kernel(group_size, grad_attn, grad_up, grad_down, mom_attn, mom_up, mom_down, mas_attn, mas_up, mas_down,
-           mo_attn, wo_attn, bo_attn, mo_up, wo_up, bo_up, mo_down, wo_down, bo_down,
+def kernel(group_size, grad_attn, grad_up, grad_down, mom_attn, mom_up, mom_down,
+           mo_attn, mo_up, mo_down, got_attn, got_up, got_down,
            own, peer, full, recv0, recv1, recv2, mom_pk, swap_attn, swap_up, swap_down,
-           send_attn, send_up, send_down, got_attn, got_up, got_down, x_mat, a_mat, b_mat, turn,
+           send_attn, send_up, send_down, x_mat, a_mat, b_mat, turn,
            load_sem, push_sem, pull_sem, rs_send, rs_recv, ag_send, ag_recv, ex_send, ex_recv):
     me = lax.axis_index('data')
     core = lax.rem(me, 2)
@@ -316,36 +316,30 @@
     def advance(x_val, y_val):
         return (COEF_A * x_val.astype(F32) + y_val.astype(BF16).astype(F32)).astype(BF16)
 
+    def symmetric(out, base, size, block):
+        for j in range(0, size, TILE):
+            val = block(j)
+            out[pl.ds(base + j, size - j), pl.ds(j, TILE)] = val
+            if j + TILE < size:
+                out[pl.ds(base + j, TILE), pl.ds(j + TILE, size - j - TILE)] = jnp.transpose(val[TILE:])
+
     def gram(base, size):
-        rows = pl.ds(base, size)
-
-        def body(j, carry):
-            off = pl.multiple_of(j * TILE, TILE)
-            a_val = lax.dot_general(x_mat[rows, :], x_mat[aligned(base + off, TILE), :], (((1,), (1,)), ((), ())),
-                                    preferred_element_type=F32)
-            a_mat[rows, pl.ds(off, TILE)] = a_val.astype(BF16)
-            return carry
-        lax.fori_loop(0, size // TILE, body, 0)
+        def block(j):
+            return lax.dot_general(x_mat[pl.ds(base + j, size - j), :], x_mat[pl.ds(base + j, TILE), :], (((1,), (1,)), ((), ())),
+                                   preferred_element_type=F32).astype(BF16)
+        symmetric(a_mat, base, size, block)
 
     def poly(base, size):
-        rows = pl.ds(base, size)
-
-        def body(j, carry):
-            cols = aligned(j * TILE, TILE)
-            q_val = jnp.dot(a_mat[rows, 0:size], a_mat[rows, cols], preferred_element_type=F32)
-            b_mat[rows, cols] = weighted(a_mat[rows, cols], q_val)
-            return carry
-        lax.fori_loop(0, size // TILE, body, 0)
+        def block(j):
+            rows, cols = pl.ds(base + j, size - j), pl.ds(j, TILE)
+            q_val = jnp.dot(a_mat[rows, pl.ds(0, size)], a_mat[pl.ds(base, size), cols], preferred_element_type=F32)
+            return weighted(a_mat[rows, cols], q_val)
+        symmetric(b_mat, base, size, block)
 
     def update(base, size):
         rows = pl.ds(base, size)
-
-        def body(j, carry):
-            cols = aligned(j * TILE, TILE)
-            y_val = jnp.dot(b_mat[rows, 0:size], x_mat[rows, cols], preferred_element_type=F32)
-            x_mat[rows, cols] = advance(x_mat[rows, cols], y_val)
-            return carry
-        lax.fori_loop(0, 4, body, 0)
+        y_val = jnp.dot(b_mat[rows, pl.ds(0, size)], x_mat[rows, :], preferred_element_type=F32)
+        x_mat[rows, :] = advance(x_mat[rows, :], y_val)
 
     def square_sum(cols):
         def body(k, acc):
@@ -403,18 +397,14 @@
             return carry
         lax.fori_loop(0, 32, fill_down, 0)
 
-        def matrix(t, carry):
-            base = pl.multiple_of(t * NARROW, NARROW)
-
-            def step(_, carry):
-                gram(base, NARROW)
-                poly(base, NARROW)
-                update(base, NARROW)
-                return carry
-            lax.fori_loop(0, NS_STEPS - 1, step, 0)
-            gram(base, NARROW)
+        def step(_, carry):
+            for stage in (gram, poly, update):
+                stage(0, NARROW)
+                stage(NARROW, NARROW)
             return carry
-        lax.fori_loop(0, 2, matrix, 0)
+        lax.fori_loop(0, NS_STEPS - 1, step, 0)
+        gram(0, NARROW)
+        gram(NARROW, NARROW)
         poly(0, NARROW)
         cols = aligned(chip // 8 * 128, 128)
         out_up = advance(x_mat[WEST, cols], jnp.dot(b_mat[WEST, WEST], x_mat[WEST, cols], preferred_element_type=F32))
@@ -444,13 +434,6 @@
         for copy in back_from_0(2, mo_attn) + back_from_0(4, got_attn):
             copy.wait_recv()
 
-    for mas, got, w_out, b_out in ((mas_attn, got_attn, wo_attn, bo_attn), (mas_up, got_up, wo_up, bo_up),
-                                   (mas_down, got_down, wo_down, bo_down)):
-        old = mas[...]
-        new = old - LEARN_RATE * (0.2 * math.sqrt(WIDE) * got[...] + WEIGHT_DECAY * old)
-        w_out[...] = new
-        b_out[...] = new.astype(BF16)
-
     @pl.when(core == 0)
     def _():
         for turn_idx in range(SIDE):
@@ -475,6 +458,17 @@
                 ag_copy(phase, color, piece).wait_send()
 
 
+def finish(*refs):
+    for k in range(3):
+        mom, out, mas = refs[k], refs[3 + k], refs[6 + k]
+        mom_out, mas_out, low_out = refs[9 + 3 * k:12 + 3 * k]
+        old = mas[...]
+        new = old - LEARN_RATE * (0.2 * math.sqrt(WIDE) * out[...] + WEIGHT_DECAY * old)
+        mom_out[...] = mom[...]
+        mas_out[...] = new
+        low_out[...] = new.astype(BF16)
+
+
 def solution(mesh):
     group_size = mesh.shape['data']
     grad_spec = P(('stage', 'data'), None, None, None)
@@ -484,15 +478,12 @@
         vmem = pl.BlockSpec(memory_space=pltpu.VMEM)
         hbm = pl.BlockSpec(memory_space=pl.ANY)
         shapes = ((8, WIDE), (8, NARROW), (SIDE, WIDE))
-        outs = []
-        for shape in shapes:
-            outs += [jax.ShapeDtypeStruct(shape, F32), jax.ShapeDtypeStruct(shape, F32), jax.ShapeDtypeStruct(shape, BF16)]
         sem = pltpu.SemaphoreType.DMA
         scratch = [
             *[pltpu.VMEM(BLOCK, F32)] * 3,
             *[pltpu.VMEM((6,) + (SIDE,) * free + (8, WIDE), F32) for free in (2, 1, 0)],
             pltpu.VMEM((CHIP_ROWS, WIDE), F32),
-            *[pltpu.VMEM(shape, F32) for shape in shapes * 3],
+            *[pltpu.VMEM(shape, F32) for shape in shapes * 2],
             *[pltpu.VMEM((WIDE, WIDE), BF16)] * 3,
             pltpu.VMEM((128, NARROW), F32),
             *[sem((3, SIDE, 3))] * 3,
@@ -501,15 +492,18 @@
         ]
         result = pl.pallas_call(
             functools.partial(kernel, group_size),
-            out_shape=outs,
-            in_specs=[hbm] * 3 + [vmem] * 6,
-            out_specs=[vmem] * 9,
+            out_shape=[jax.ShapeDtypeStruct(shape, F32) for shape in shapes * 2],
+            in_specs=[hbm] * 3 + [vmem] * 3,
+            out_specs=[vmem] * 6,
             scratch_shapes=scratch,
             compiler_params=pltpu.CompilerParams(collective_id=0, has_side_effects=True, vmem_limit_bytes=60 * 1024 * 1024),
             name='muon',
         )(grad_attn.reshape(BLOCK), grad_up.reshape(BLOCK[:4] + (NARROW,)), grad_down.reshape(BLOCK[:3] + (8, WIDE)),
-          *(v[0] for v in (mom_attn, mom_up, mom_down, mas_attn, mas_up, mas_down)))
-        return tuple(r[None] for r in result)
+          mom_attn[0], mom_up[0], mom_down[0])
+        outs = [jax.ShapeDtypeStruct(shape, dtype) for shape in shapes for dtype in (F32, F32, BF16)]
+        done = pl.pallas_call(finish, out_shape=outs, in_specs=[vmem] * 9, out_specs=[vmem] * 9, name='finish')(
+            *result, mas_attn[0], mas_up[0], mas_down[0])
+        return tuple(d[None] for d in done)
 
     return jax.shard_map(step_local, mesh=mesh, in_specs=(grad_spec, row_spec, row_spec) * 3, out_specs=(row_spec,) * 9,
                          check_vma=False)

time: 125 us -> 97.8 us (0.78)
  Pallas kernels: 111 us -> 96.9 us
  local copies, waits for them, and re-layouts: 12 us -> 0 us
    pallas_call x1 -> x2, Pallas kernels: 111 us -> 96.9 us  [the longest x1 95.3 us: step_local(): pl.pallas_call(functools.partial(kernel, group_size), out_shape=[jax.Shap...]
    unnamed x9 -> x0, local copies, waits for them, and re-layouts: 12 us -> none
where the time goes in v2:
time: 97.8 us; the launch traced here: 97.5 us
  Pallas kernels  96.9 us (99%)
    pallas_call x1, Pallas kernels, step_local(): pl.pallas_call(functools.partial(kernel, group_size), out_shape=[jax.Shap...  95.3 us

profile of v2, /device:TPU:1, one launch (start us, length us, event | category | flops | bytes accessed | tf_op | source)
XLA Modules:
  0.0 97.5 jit_solution(15234056070287142753)
XLA Ops:
  0.6 95.3 %muon.1 = (f32[8,1024]{1,0:T(8,128)}, f32[8,512]{1,0:T(8,128)}, f32[4,1024]{1,0:T(4,128)}, f32[8,1024]{1,0:T(8,128)}, f32[8,512]{1,0:T(8,128)}, /*index=5*/f32[4,1024]{1,0:T(4,128)}) custom-call(f32[4,4,4,16,1024]{4,3,2,1,0:T(8,128)} %bitcast.18, f32[4,4,4,16,512]{4,3,2,1,0:T(8,128)} %bitcast.19, f32[4,4,4,8,1024]{4,3,2,1,0:T(8,128)} %bitcast.20, ...), custom_call_target="tpu_custom_call" | custom-call | tf_op jit(solution)/shard_map/muon/pallas_call | solution.py:493
  96.0 1.6 %finish.1 = (f32[8,1024]{1,0:T(8,128)}, f32[8,1024]{1,0:T(8,128)}, bf16[8,1024]{1,0:T(8,128)(2,1)}, f32[8,512]{1,0:T(8,128)}, f32[8,512]{1,0:T(8,128)}, /*index=...) custom-call(f32[8,1024]{1,0:T(8,128)} %get-tuple-element.24.refs_0_, ...), custom_call_target="tpu_custom_call" | custom-call | tf_op jit(solution)/shard_map/finish/pallas_call | solution.py:504

commit v3 on v2

v3 whole, which is shorter than its diff:
```python
import functools
import math

import jax
import jax.numpy as jnp
from jax import lax
from jax.experimental import pallas as pl
from jax.experimental.pallas import tpu as pltpu
from jax.sharding import PartitionSpec as P

MOMENTUM = 0.95
LEARN_RATE = 0.25
WEIGHT_DECAY = 0.2
EPSILON = 1e-7
COEF_A = 3.4445
COEF_B = -4.7750
COEF_C = 2.0315
NS_STEPS = 5

F32 = jnp.float32
BF16 = jnp.bfloat16

COLS = ((0, 384), (384, 384), (768, 256))
ORDER = ((0, 1, 2), (1, 2, 0), (2, 0, 1))
ATTN = 1
EXPERT = 0
SIDE = 4
CHIP_ROWS = 16
WIDE = 1024
NARROW = 512
TILE = 256
BLOCK = (SIDE, SIDE, SIDE, CHIP_ROWS, WIDE)
ALL = slice(None)
LO = pl.ds(0, 8)
HI = pl.ds(8, 8)
HALF = (LO, HI)
WEST = pl.ds(0, NARROW)
EAST = pl.ds(NARROW, NARROW)
PIECES = (
    (('up', 0, 384, ALL, 0),),
    (('up', 384, 128, ALL, 384), ('down', 0, TILE, LO, NARROW), ('down', NARROW, TILE, HI, NARROW)),
    (('down', TILE, TILE, LO, 768), ('down', 768, TILE, HI, 768)),
)


def place(ref, fixed, rows, cols):
    return ref.at[region(fixed, rows, cols)]


def region(fixed, rows, cols):
    return tuple(fixed.get(axis, ALL) for axis in range(3)) + (rows, cols)


def coords_of(k):
    return k // (SIDE * SIDE), lax.rem(k // SIDE, SIDE), lax.rem(k, SIDE)


def aligned(start, size):
    return pl.ds(pl.multiple_of(start, size), size)


def kernel(group_size, grad_attn, grad_up, grad_down, mom_attn, mom_up, mom_down,
           mo_attn, mo_up, mo_down, got_attn, got_up, got_down,
           own, peer, full, recv0, recv1, recv2, mom_pk, swap_attn, swap_up, swap_down, keep_attn, keep_up, keep_down,
           send_attn, send_up, send_down, x_mat, a_mat, b_mat, turn, x_all, norms, scales,
           load_sem, push_sem, pull_sem, rs_send, rs_recv, ag_send, ag_recv, ex_send, ex_recv, keep_sem, norm_send, norm_recv, gate):
    me = lax.axis_index('data')
    core = lax.rem(me, 2)
    chip = me // 2
    pos = coords_of(chip)
    partner = me + 1 - 2 * core
    recvs = (recv0, recv1, recv2)

    def at_axis(axis, coord):
        coords = list(pos)
        coords[axis] = coord
        return ((coords[0] * SIDE + coords[1]) * SIDE + coords[2]) * 2 + core

    right = [lax.rem(p + 1, SIDE) for p in pos]
    left = [lax.rem(p + 3, SIDE) for p in pos]
    far = [lax.rem(p + 2, SIDE) for p in pos]
    right_dev = [at_axis(a, right[a]) for a in range(3)]
    left_dev = [at_axis(a, left[a]) for a in range(3)]
    far_dev = [at_axis(a, far[a]) for a in range(3)]

    def remote(src, dst, send_sem, recv_sem, device):
        return pltpu.make_async_remote_copy(src_ref=src, dst_ref=dst, send_sem=send_sem, recv_sem=recv_sem,
                                            device_id={'data': device}, device_id_type=pl.DeviceIdType.MESH)

    def turns(color):
        axis = ORDER[color][0]
        return axis, (far[axis], right[axis], left[axis], pos[axis])

    def attn_copy(color, turn_idx, push):
        axis, coords = turns(color)
        cols = pl.ds(*COLS[color])
        src = place(grad_attn, {axis: coords[turn_idx]}, ALL, cols)
        if push:
            dst = place(peer, {axis: coords[turn_idx]}, ALL, cols)
            return remote(src, dst, push_sem.at[color, turn_idx, 0], pull_sem.at[color, turn_idx, 0], partner)
        dst = place(own, {axis: coords[turn_idx]}, ALL, cols)
        return pltpu.make_async_copy(src, dst, load_sem.at[color, turn_idx, 0])

    def expert_copies(color, turn_idx, push):
        axis, coords = turns(color)
        copies = []
        for k, (source, col, width, rows, packed) in enumerate(PIECES[color]):
            src = place(grad_up if source == 'up' else grad_down, {axis: coords[turn_idx]}, ALL, pl.ds(col, width))
            target = peer if push else own
            dst = place(target, {axis: coords[turn_idx]}, rows, pl.ds(packed, width))
            if push:
                copies.append(remote(src, dst, push_sem.at[color, turn_idx, k], pull_sem.at[color, turn_idx, k], partner))
            else:
                copies.append(pltpu.make_async_copy(src, dst, load_sem.at[color, turn_idx, k]))
        return copies

    def mom_from_attn():
        return [remote(mom_up, swap_up, ex_send.at[0], ex_recv.at[0], partner),
                remote(mom_down, swap_down, ex_send.at[1], ex_recv.at[1], partner)]

    def mom_from_expert():
        return [remote(mom_attn, swap_attn, ex_send.at[0], ex_recv.at[0], partner)]

    def keep_copies(role):
        pairs = ((mom_attn, keep_attn),) if role == ATTN else ((mom_up, keep_up), (mom_down, keep_down))
        return [pltpu.make_async_copy(src, dst, keep_sem.at[k]) for k, (src, dst) in enumerate(pairs)]

    barrier = pltpu.get_barrier_semaphore()
    for device in [partner] + right_dev + left_dev + far_dev:
        pl.semaphore_signal(barrier, inc=1, device_id={'data': device}, device_id_type=pl.DeviceIdType.MESH)

    @pl.when(core == ATTN)
    def _():
        for turn_idx in range(SIDE):
            for color in range(3):
                attn_copy(color, turn_idx, False).start()
        for copy in keep_copies(ATTN):
            copy.start()

    with jax.named_scope('barrier'):
        pl.semaphore_wait(barrier, 10)

    @pl.when(core == ATTN)
    def _():
        for copy in mom_from_attn():
            copy.start()
        for turn_idx in range(SIDE):
            for color in range(3):
                for copy in expert_copies(color, turn_idx, True):
                    copy.start()

    @pl.when(core == EXPERT)
    def _():
        for turn_idx in range(SIDE):
            for color in range(3):
                attn_copy(color, turn_idx, True).start()
        for copy in mom_from_expert():
            copy.start()
        for copy in keep_copies(EXPERT):
            copy.start()
        for turn_idx in range(SIDE):
            for color in range(3):
                for copy in expert_copies(color, turn_idx, False):
                    copy.start()
        with jax.named_scope('gate'):
            pl.semaphore_wait(gate, 1)

    def open_gate():
        @pl.when(core == ATTN)
        def _():
            pl.semaphore_signal(gate, inc=1, device_id={'data': partner}, device_id_type=pl.DeviceIdType.MESH)

    def chip_sum(color, turn_idx):
        @pl.when(core == ATTN)
        def _():
            attn_copy(color, turn_idx, False).wait()
            attn_copy(color, turn_idx, True).wait_recv()

        @pl.when(core == EXPERT)
        def _():
            for copy in expert_copies(color, turn_idx, False):
                copy.wait()
            for copy in expert_copies(color, turn_idx, True):
                copy.wait_recv()
        axis, coords = turns(color)
        idx = region({axis: coords[turn_idx]}, ALL, pl.ds(*COLS[color]))
        own[idx] = own[idx] + peer[idx]

    PAIRED = ((far, 0, right_dev), (far, 1, left_dev), (right, 1, right_dev), (left, 0, left_dev), (right, 0, right_dev), (left, 1, left_dev))
    DIRECT = ((far, far_dev), (right, right_dev), (left, left_dev))

    def ctx(phase, color):
        order = ORDER[color]
        return order[phase], {order[k]: pos[order[k]] for k in range(phase)}, pl.ds(*COLS[color])

    def rs_slot(phase, color, piece):
        return (piece,) + (ALL,) * (2 - phase) + (ALL, pl.ds(*COLS[color]))

    def rs_copy(phase, color, piece):
        axis, fixed, cols = ctx(phase, color)
        if phase < 2:
            coord, half, device = PAIRED[piece]
            rows = HALF[half]
        else:
            coord, device = DIRECT[piece]
            rows = ALL
        src = place(own, {**fixed, axis: coord[axis]}, rows, cols)
        return remote(src, recvs[phase].at[rs_slot(phase, color, piece)], rs_send.at[phase, color, piece],
                      rs_recv.at[phase, color, piece], device[axis])

    def rs_add(phase, color, coord, rows, pieces):
        axis, fixed, cols = ctx(phase, color)
        idx = region({**fixed, axis: coord[axis]}, rows, cols)
        total = own[idx]
        for piece in pieces:
            total = total + recvs[phase][rs_slot(phase, color, piece)]
        own[idx] = total

    def rs_mid(phase, color):
        rs_copy(phase, color, 0).wait_recv()
        rs_add(phase, color, right, LO, (0,))
        rs_copy(phase, color, 4).start()
        rs_copy(phase, color, 1).wait_recv()
        rs_add(phase, color, left, HI, (1,))
        rs_copy(phase, color, 5).start()

    def rs_end(phase, color):
        for piece in (2, 3, 4, 5):
            rs_copy(phase, color, piece).wait_recv()
        rs_add(phase, color, pos, LO, (3, 4))
        rs_add(phase, color, pos, HI, (2, 5))

    with jax.named_scope('rs0_load'):
        for color in range(3):
            chip_sum(color, 0)
            rs_copy(0, color, 0).start()
            rs_copy(0, color, 1).start()
        open_gate()
        for turn_idx in (1, 2):
            for color in range(3):
                chip_sum(color, turn_idx)
                rs_copy(0, color, turn_idx + 1).start()
    with jax.named_scope('rs0_mid'):
        for color in range(3):
            rs_mid(0, color)
        for color in range(3):
            chip_sum(color, 3)
    with jax.named_scope('rs0_end'):
        for color in range(3):
            rs_end(0, color)
            for piece in range(4):
                rs_copy(1, color, piece).start()
    with jax.named_scope('rs1_mid'):
        for color in range(3):
            rs_mid(1, color)
    with jax.named_scope('rs1_end'):
        for color in range(3):
            rs_end(1, color)
            for piece in range(3):
                rs_copy(2, color, piece).start()
    with jax.named_scope('rs2'):
        for color in range(3):
            for piece in range(3):
                rs_copy(2, color, piece).wait_recv()
            rs_add(2, color, pos, ALL, range(3))

    @pl.when(core == ATTN)
    def _():
        mom_from_expert()[0].wait_recv()
        keep_copies(ATTN)[0].wait()
        mom_pk[LO] = swap_attn[...]
        mom_pk[HI] = keep_attn[...]

    @pl.when(core == EXPERT)
    def _():
        for copy in mom_from_attn():
            copy.wait_recv()
        for copy in keep_copies(EXPERT):
            copy.wait()
        mom_pk[LO, WEST] = keep_up[...]
        mom_pk[HI, WEST] = swap_up[...]
        for first, cols in ((0, WEST), (8, EAST)):
            mom_pk[pl.ds(first, SIDE), EAST] = keep_down[:, cols]
            mom_pk[pl.ds(first + SIDE, SIDE), EAST] = swap_down[:, cols]

    mine = pos
    mom_new = MOMENTUM * mom_pk[...] + own[mine] * (1.0 / group_size)
    full[mine] = mom_new

    AG_SEND = ((pos, 0, right_dev), (pos, 1, left_dev), (pos, 1, right_dev), (pos, 0, left_dev), (left, 0, right_dev), (right, 1, left_dev))
    AG_LAND = ((left, 0), (right, 1), (left, 1), (right, 0), (far, 0), (far, 1))
    AG_DIRECT = (far, left, right)

    def ag_part(phase, color, coord, rows):
        axis, fixed, cols = ctx(phase, color)
        return place(full, {**fixed, axis: coord[axis]}, rows, cols)

    def ag_half(phase, color, coord, half):
        if phase == 1:
            return ag_part(phase, color, coord, HALF[half])
        axis, second, _ = ORDER[color]
        return place(x_all, {axis: coord[axis], second: pl.ds(2 * half, 2)}, ALL, pl.ds(*COLS[color]))

    def ag_remote(part, phase, color, piece, device):
        return remote(part, part, ag_send.at[phase, color, piece], ag_recv.at[phase, color, piece], device[ORDER[color][phase]])

    def ag_copy(phase, color, piece):
        if phase < 2:
            coord, half, device = AG_SEND[piece]
            return ag_remote(ag_half(phase, color, coord, half), phase, color, piece, device)
        return ag_remote(ag_part(phase, color, pos, ALL), phase, color, piece, DIRECT[piece][1])

    def ag_arrive(phase, color, piece):
        if phase < 2:
            coord, half = AG_LAND[piece]
            part = ag_half(phase, color, coord, half)
        else:
            part = ag_part(phase, color, AG_DIRECT[piece], ALL)
        ag_remote(part, phase, color, piece, right_dev).wait_recv()

    def drain_push():
        @pl.when(core == ATTN)
        def _():
            for turn_idx in range(SIDE):
                for color in range(3):
                    for copy in expert_copies(color, turn_idx, True):
                        copy.wait_send()
            for copy in mom_from_attn():
                copy.wait_send()

        @pl.when(core == EXPERT)
        def _():
            for turn_idx in range(SIDE):
                for color in range(3):
                    attn_copy(color, turn_idx, True).wait_send()
            for copy in mom_from_expert():
                copy.wait_send()

    with jax.named_scope('ag2'):
        for color in range(3):
            for piece in range(3):
                ag_copy(2, color, piece).start()
        drain_push()
        for color in range(3):
            for piece in range(3):
                ag_arrive(2, color, piece)
            for piece in range(4):
                ag_copy(1, color, piece).start()
    def drain(phase, make):
        for color in range(3):
            for piece in range(6 if phase < 2 else 3):
                make(phase, color, piece).wait_send()

    def ag_mid(phase):
        for color in range(3):
            ag_arrive(phase, color, 0)
            ag_copy(phase, color, 4).start()
            ag_arrive(phase, color, 1)
            ag_copy(phase, color, 5).start()

    def norm_copy(color, piece):
        axis = ORDER[color][0]
        part = norms.at[color, pos[axis]]
        return remote(part, part, norm_send.at[color, piece], norm_recv.at[color, piece], DIRECT[piece][1][axis])

    def norm_arrive(color, piece):
        axis = ORDER[color][0]
        part = norms.at[color, AG_DIRECT[piece][axis]]
        remote(part, part, norm_send.at[color, piece], norm_recv.at[color, piece], right_dev[axis]).wait_recv()

    def square_tile(plane, cols):
        val = full[plane + (ALL, cols)].reshape(32, 8, cols.size)
        val = jnp.sum(val * val, axis=0)
        return sum(val[:, k:k + 128] for k in range(0, cols.size, 128))

    def norm_start(color):
        axis = ORDER[color][0]
        plane = region({axis: pos[axis]}, ALL, ALL)[:3]
        first, width = COLS[color]
        west = max(0, min(NARROW - first, width))
        for side, (start, size) in enumerate(((first, west), (first + west, width - west))):
            val = square_tile(plane, pl.ds(start, size)) if size else jnp.zeros((8, 128), F32)
            norms[color, pos[axis], side] = val
        for piece in range(3):
            norm_copy(color, piece).start()

    drain(1, rs_copy)
    drain(2, ag_copy)
    with jax.named_scope('ag1_mid'):
        ag_mid(1)
    with jax.named_scope('ag1_end'):
        for color in range(3):
            for piece in (2, 3, 4, 5):
                ag_arrive(1, color, piece)
            norm_start(color)
    drain(0, rs_copy)
    drain(2, rs_copy)
    drain(1, ag_copy)
    with jax.named_scope('norm'):
        for color in range(3):
            for piece in range(3):
                norm_arrive(color, piece)
        tiles = [norms[color, j] for color in range(3) for j in range(SIDE)]
        total = jnp.sum(sum(tiles), axis=(1, 2), keepdims=True)
        west, east = total[0], total[1]
        both = west + east
        west = jnp.where(core == ATTN, both, west)
        east = jnp.where(core == ATTN, both, east)
        lane = lax.broadcasted_iota(jnp.int32, (1, WIDE), 1)
        norm = jnp.sqrt(jnp.where(lane < NARROW, west, east))
        scales[...] = 1.0 / (norm + EPSILON)
    with jax.named_scope('ag0_start'):
        for color in range(3):
            axis, cols = ORDER[color][0], pl.ds(*COLS[color])
            idx = region({axis: pos[axis]}, ALL, cols)
            x_all[idx] = (full[idx] * scales[:, cols]).astype(BF16)
            for piece in range(4):
                ag_copy(0, color, piece).start()
    with jax.named_scope('ag0_mid'):
        ag_mid(0)
    with jax.named_scope('ag0_end'):
        for color in range(3):
            for piece in (2, 3, 4, 5):
                ag_arrive(0, color, piece)
    for color in range(3):
        for piece in range(3):
            norm_copy(color, piece).wait_send()
    drain(0, ag_copy)

    @pl.when(core == ATTN)
    def _():
        send_attn[...] = full[mine + (LO, ALL)]
        mo_attn[...] = full[mine + (HI, ALL)]

    @pl.when(core == EXPERT)
    def _():
        send_up[...] = full[mine + (HI, WEST)]
        mo_up[...] = full[mine + (LO, WEST)]
        for rows, cols in ((LO, WEST), (HI, EAST)):
            down = full[mine + (rows, EAST)]
            send_down[:, cols] = down[SIDE:]
            mo_down[:, cols] = down[:SIDE]

    def back_from_attn(base, out_attn):
        return [remote(send_attn, out_attn, ex_send.at[base], ex_recv.at[base], partner)]

    def back_from_expert(base, out_up, out_down):
        return [remote(send_up, out_up, ex_send.at[base], ex_recv.at[base], partner),
                remote(send_down, out_down, ex_send.at[base + 1], ex_recv.at[base + 1], partner)]

    @pl.when(core == ATTN)
    def _():
        for copy in back_from_attn(2, mo_attn):
            copy.start()

    @pl.when(core == EXPERT)
    def _():
        for copy in back_from_expert(2, mo_up, mo_down):
            copy.start()

    def weighted(a_val, q_val):
        return (COEF_B * a_val.astype(F32) + COEF_C * q_val.astype(BF16).astype(F32)).astype(BF16)

    def advance(x_val, y_val):
        return (COEF_A * x_val.astype(F32) + y_val.astype(BF16).astype(F32)).astype(BF16)

    def symmetric(out, base, size, block):
        for j in range(0, size, TILE):
            val = block(j)
            out[pl.ds(base + j, size - j), pl.ds(j, TILE)] = val
            if j + TILE < size:
                out[pl.ds(base + j, TILE), pl.ds(j + TILE, size - j - TILE)] = jnp.transpose(val[TILE:])

    def gram(base, size):
        def block(j):
            return lax.dot_general(x_mat[pl.ds(base + j, size - j), :], x_mat[pl.ds(base + j, TILE), :], (((1,), (1,)), ((), ())),
                                   preferred_element_type=F32).astype(BF16)
        symmetric(a_mat, base, size, block)

    def poly(base, size):
        def block(j):
            rows, cols = pl.ds(base + j, size - j), pl.ds(j, TILE)
            q_val = jnp.dot(a_mat[rows, pl.ds(0, size)], a_mat[pl.ds(base, size), cols], preferred_element_type=F32)
            return weighted(a_mat[rows, cols], q_val)
        symmetric(b_mat, base, size, block)

    def update(base, size):
        rows = pl.ds(base, size)
        y_val = jnp.dot(b_mat[rows, pl.ds(0, size)], x_mat[rows, :], preferred_element_type=F32)
        x_mat[rows, :] = advance(x_mat[rows, :], y_val)

    @pl.when(core == ATTN)
    def _():
        with jax.named_scope('fill'):
            x_mat[...] = x_all[...].reshape(WIDE, WIDE)

        def step(_, carry):
            gram(0, WIDE)
            poly(0, WIDE)
            update(0, WIDE)
            return carry
        with jax.named_scope('steps'):
            lax.fori_loop(0, NS_STEPS - 1, step, 0)
            gram(0, WIDE)
        rows = aligned(chip * CHIP_ROWS, CHIP_ROWS)
        a_val = a_mat[rows, :]
        b_val = weighted(a_val, jnp.dot(a_val, a_mat[...], preferred_element_type=F32))
        out = advance(x_mat[rows, :], jnp.dot(b_val, x_mat[...], preferred_element_type=F32)).astype(F32)
        back_from_attn(2, mo_attn)[0].wait_send()
        send_attn[...] = out[:8]
        got_attn[...] = out[8:]
        back_from_attn(4, got_attn)[0].start()

    @pl.when(core == EXPERT)
    def _():
        with jax.named_scope('fill'):
            def fill_up(k, carry):
                val = x_all[k // 2, pl.ds(2 * lax.rem(k, 2), 2), :, :, WEST].reshape(128, NARROW)
                x_mat[WEST, aligned(k * 128, 128)] = jnp.transpose(val)
                return carry
            lax.fori_loop(0, 8, fill_up, 0)

            def fill_down(k, carry):
                z, y, x = coords_of(2 * k)
                val = x_all[z, y, pl.ds(x, 2), :, EAST].astype(F32)
                rows = aligned(NARROW + k * CHIP_ROWS, CHIP_ROWS)
                x_mat[rows, WEST] = val[:, :8].reshape(CHIP_ROWS, NARROW).astype(BF16)
                x_mat[rows, EAST] = val[:, 8:].reshape(CHIP_ROWS, NARROW).astype(BF16)
                return carry
            lax.fori_loop(0, 32, fill_down, 0)

        def step(_, carry):
            for stage in (gram, poly, update):
                stage(0, NARROW)
                stage(NARROW, NARROW)
            return carry
        with jax.named_scope('steps'):
            lax.fori_loop(0, NS_STEPS - 1, step, 0)
            gram(0, NARROW)
            gram(NARROW, NARROW)
        poly(0, NARROW)
        cols = aligned(chip // 8 * 128, 128)
        out_up = advance(x_mat[WEST, cols], jnp.dot(b_mat[WEST, WEST], x_mat[WEST, cols], preferred_element_type=F32))
        turn[...] = jnp.transpose(out_up.astype(F32))
        rows = aligned(NARROW + chip // 2 * CHIP_ROWS, CHIP_ROWS)
        a_val = a_mat[rows, WEST]
        b_val = weighted(a_val, jnp.dot(a_val, a_mat[EAST, WEST], preferred_element_type=F32))
        both = advance(x_mat[rows, :], jnp.dot(b_val, x_mat[EAST, :], preferred_element_type=F32)).astype(F32)
        out_down = jnp.where(lax.rem(chip, 2) == 0, both[:8], both[8:])
        for copy in back_from_expert(2, mo_up, mo_down):
            copy.wait_send()
        first = pl.multiple_of(lax.rem(chip, 8) * CHIP_ROWS, CHIP_ROWS)
        send_up[...] = turn[pl.ds(first + 8, 8), :]
        got_up[...] = turn[pl.ds(first, 8), :]
        send_down[...] = out_down[SIDE:]
        got_down[...] = out_down[:SIDE]
        for copy in back_from_expert(4, got_up, got_down):
            copy.start()

    @pl.when(core == ATTN)
    def _():
        for copy in back_from_expert(2, mo_up, mo_down) + back_from_expert(4, got_up, got_down):
            copy.wait_recv()

    @pl.when(core == EXPERT)
    def _():
        for copy in back_from_attn(2, mo_attn) + back_from_attn(4, got_attn):
            copy.wait_recv()

    @pl.when(core == ATTN)
    def _():
        for copy in back_from_attn(4, got_attn):
            copy.wait_send()

    @pl.when(core == EXPERT)
    def _():
        for copy in back_from_expert(4, got_up, got_down):
            copy.wait_send()


def finish(*refs):
    for k in range(3):
        mom, out, mas = refs[k], refs[3 + k], refs[6 + k]
        mom_out, mas_out, low_out = refs[9 + 3 * k:12 + 3 * k]
        old = mas[...]
        new = old - LEARN_RATE * (0.2 * math.sqrt(WIDE) * out[...] + WEIGHT_DECAY * old)
        mom_out[...] = mom[...]
        mas_out[...] = new
        low_out[...] = new.astype(BF16)


def solution(mesh):
    group_size = mesh.shape['data']
    grad_spec = P(('stage', 'data'), None, None, None)
    row_spec = P('stage', 'data', None)

    def step_local(grad_attn, mom_attn, mas_attn, grad_up, mom_up, mas_up, grad_down, mom_down, mas_down):
        vmem = pl.BlockSpec(memory_space=pltpu.VMEM)
        hbm = pl.BlockSpec(memory_space=pl.ANY)
        shapes = ((8, WIDE), (8, NARROW), (SIDE, WIDE))
        sem = pltpu.SemaphoreType.DMA
        scratch = [
            *[pltpu.VMEM(BLOCK, F32)] * 3,
            *[pltpu.VMEM((6,) + (SIDE,) * free + (8, WIDE), F32) for free in (2, 1)],
            pltpu.VMEM((3, CHIP_ROWS, WIDE), F32),
            pltpu.VMEM((CHIP_ROWS, WIDE), F32),
            *[pltpu.VMEM(shape, F32) for shape in shapes * 3],
            *[pltpu.VMEM((WIDE, WIDE), BF16)] * 3,
            pltpu.VMEM((128, NARROW), F32),
            pltpu.VMEM(BLOCK, BF16), pltpu.VMEM((3, SIDE, 2, 8, 128), F32), pltpu.VMEM((1, WIDE), F32),
            *[sem((3, SIDE, 3))] * 3,
            *[sem((3, 3, 6))] * 4,
            *[sem((6,))] * 2,
            sem((2,)),
            *[sem((3, 3))] * 2,
            pltpu.SemaphoreType.REGULAR,
        ]
        result = pl.pallas_call(
            functools.partial(kernel, group_size),
            out_shape=[jax.ShapeDtypeStruct(shape, F32) for shape in shapes * 2],
            in_specs=[hbm] * 6,
            out_specs=[vmem] * 6,
            scratch_shapes=scratch,
            compiler_params=pltpu.CompilerParams(collective_id=0, has_side_effects=True, vmem_limit_bytes=60 * 1024 * 1024),
            name='muon',
        )(grad_attn.reshape(BLOCK), grad_up.reshape(BLOCK[:4] + (NARROW,)), grad_down.reshape(BLOCK[:3] + (8, WIDE)),
          mom_attn[0], mom_up[0], mom_down[0])
        outs = [jax.ShapeDtypeStruct(shape, dtype) for shape in shapes for dtype in (F32, F32, BF16)]
        done = pl.pallas_call(finish, out_shape=outs, in_specs=[vmem] * 9, out_specs=[vmem] * 9, name='finish')(
            *result, mas_attn[0], mas_up[0], mas_down[0])
        return tuple(d[None] for d in done)

    return jax.shard_map(step_local, mesh=mesh, in_specs=(grad_spec, row_spec, row_spec) * 3, out_specs=(row_spec,) * 9,
                         check_vma=False)
```

time: 97.8 us -> 83 us (0.85)
  Pallas kernels: 96.9 us -> 82 us
    pallas_call x1, Pallas kernels: 95.3 us -> 80.4 us  [step_local(): pl.pallas_call(functools.partial(kernel, group_size), out_shape=[jax.Shap...]
where the time goes in v3:
time: 83 us; the launch traced here: 82.8 us
  Pallas kernels  82 us (99%)
    pallas_call x1, Pallas kernels, step_local(): pl.pallas_call(functools.partial(kernel, group_size), out_shape=[jax.Shap...  80.4 us

profile of v3, /device:TPU:1, one launch (start us, length us, event | category | flops | bytes accessed | tf_op | source)
XLA Modules:
  0.0 82.8 jit_solution(4914224689892005233)
XLA Ops:
  0.6 80.4 %muon.1 = (f32[8,1024]{1,0:T(8,128)}, f32[8,512]{1,0:T(8,128)}, f32[4,1024]{1,0:T(4,128)}, f32[8,1024]{1,0:T(8,128)}, f32[8,512]{1,0:T(8,128)}, /*index=5*/f32[4,1024]{1,0:T(4,128)}) custom-call(f32[4,4,4,16,1024]{4,3,2,1,0:T(8,128)} %bitcast.18, f32[4,4,4,16,512]{4,3,2,1,0:T(8,128)} %bitcast.19, f32[4,4,4,8,1024]{4,3,2,1,0:T(8,128)} %bitcast.20, ...), custom_call_target="tpu_custom_call" | custom-call | tf_op jit(solution)/shard_map/muon/pallas_call | solution.py:618
  81.1 1.6 %finish.1 = (f32[8,1024]{1,0:T(8,128)}, f32[8,1024]{1,0:T(8,128)}, bf16[8,1024]{1,0:T(8,128)(2,1)}, f32[8,512]{1,0:T(8,128)}, f32[8,512]{1,0:T(8,128)}, /*index=...) custom-call(f32[8,1024]{1,0:T(8,128)} %get-tuple-element.24.refs_0_, ...), custom_call_target="tpu_custom_call" | custom-call | tf_op jit(solution)/shard_map/finish/pallas_call | solution.py:629

commit v4 on v3

--- a/solution.py
+++ b/solution.py
@@ -62,8 +62,8 @@
 def kernel(group_size, grad_attn, grad_up, grad_down, mom_attn, mom_up, mom_down,
            mo_attn, mo_up, mo_down, got_attn, got_up, got_down,
            own, peer, full, recv0, recv1, recv2, mom_pk, swap_attn, swap_up, swap_down, keep_attn, keep_up, keep_down,
-           send_attn, send_up, send_down, x_mat, a_mat, b_mat, turn, x_all, norms, scales,
-           load_sem, push_sem, pull_sem, rs_send, rs_recv, ag_send, ag_recv, ex_send, ex_recv, keep_sem, norm_send, norm_recv, gate):
+           send_down, stay_down, out_pk, x_mat, a_mat, b_mat, turn, x_all, norms, scales,
+           load_sem, push_sem, pull_sem, rs_send, rs_recv, ag_send, ag_recv, ex_send, ex_recv, back_send, back_recv, stay_sem, keep_sem, norm_send, norm_recv, gate):
     me = lax.axis_index('data')
     core = lax.rem(me, 2)
     chip = me // 2
@@ -87,6 +87,12 @@
         return pltpu.make_async_remote_copy(src_ref=src, dst_ref=dst, send_sem=send_sem, recv_sem=recv_sem,
                                             device_id={'data': device}, device_id_type=pl.DeviceIdType.MESH)
 
+    def arrived(part, sem):
+        remote(part, part, sem, sem, partner).wait_recv()
+
+    def departed(part, sem):
+        remote(part, part, sem, sem, partner).wait_send()
+
     def turns(color):
         axis = ORDER[color][0]
         return axis, (far[axis], right[axis], left[axis], pos[axis])
@@ -97,21 +103,21 @@
         src = place(grad_attn, {axis: coords[turn_idx]}, ALL, cols)
         if push:
             dst = place(peer, {axis: coords[turn_idx]}, ALL, cols)
-            return remote(src, dst, push_sem.at[color, turn_idx, 0], pull_sem.at[color, turn_idx, 0], partner)
+            return remote(src, dst, push_sem, pull_sem.at[color, turn_idx], partner)
         dst = place(own, {axis: coords[turn_idx]}, ALL, cols)
-        return pltpu.make_async_copy(src, dst, load_sem.at[color, turn_idx, 0])
+        return pltpu.make_async_copy(src, dst, load_sem.at[color, turn_idx])
 
     def expert_copies(color, turn_idx, push):
         axis, coords = turns(color)
         copies = []
-        for k, (source, col, width, rows, packed) in enumerate(PIECES[color]):
+        for source, col, width, rows, packed in PIECES[color]:
             src = place(grad_up if source == 'up' else grad_down, {axis: coords[turn_idx]}, ALL, pl.ds(col, width))
             target = peer if push else own
             dst = place(target, {axis: coords[turn_idx]}, rows, pl.ds(packed, width))
             if push:
-                copies.append(remote(src, dst, push_sem.at[color, turn_idx, k], pull_sem.at[color, turn_idx, k], partner))
+                copies.append(remote(src, dst, push_sem, pull_sem.at[color, turn_idx], partner))
             else:
-                copies.append(pltpu.make_async_copy(src, dst, load_sem.at[color, turn_idx, k]))
+                copies.append(pltpu.make_async_copy(src, dst, load_sem.at[color, turn_idx]))
         return copies
 
     def mom_from_attn():
@@ -126,7 +132,7 @@
         return [pltpu.make_async_copy(src, dst, keep_sem.at[k]) for k, (src, dst) in enumerate(pairs)]
 
     barrier = pltpu.get_barrier_semaphore()
-    for device in [partner] + right_dev + left_dev + far_dev:
+    for device in [partner] + right_dev + left_dev:
         pl.semaphore_signal(barrier, inc=1, device_id={'data': device}, device_id_type=pl.DeviceIdType.MESH)
 
     @pl.when(core == ATTN)
@@ -138,7 +144,7 @@
             copy.start()
 
     with jax.named_scope('barrier'):
-        pl.semaphore_wait(barrier, 10)
+        pl.semaphore_wait(barrier, 7)
 
     @pl.when(core == ATTN)
     def _():
@@ -171,19 +177,10 @@
             pl.semaphore_signal(gate, inc=1, device_id={'data': partner}, device_id_type=pl.DeviceIdType.MESH)
 
     def chip_sum(color, turn_idx):
-        @pl.when(core == ATTN)
-        def _():
-            attn_copy(color, turn_idx, False).wait()
-            attn_copy(color, turn_idx, True).wait_recv()
-
-        @pl.when(core == EXPERT)
-        def _():
-            for copy in expert_copies(color, turn_idx, False):
-                copy.wait()
-            for copy in expert_copies(color, turn_idx, True):
-                copy.wait_recv()
         axis, coords = turns(color)
         idx = region({axis: coords[turn_idx]}, ALL, pl.ds(*COLS[color]))
+        pltpu.make_async_copy(own.at[idx], own.at[idx], load_sem.at[color, turn_idx]).wait()
+        arrived(peer.at[idx], pull_sem.at[color, turn_idx])
         own[idx] = own[idx] + peer[idx]
 
     PAIRED = ((far, 0, right_dev), (far, 1, left_dev), (right, 1, right_dev), (left, 0, left_dev), (right, 0, right_dev), (left, 1, left_dev))
@@ -205,8 +202,16 @@
             coord, device = DIRECT[piece]
             rows = ALL
         src = place(own, {**fixed, axis: coord[axis]}, rows, cols)
-        return remote(src, recvs[phase].at[rs_slot(phase, color, piece)], rs_send.at[phase, color, piece],
-                      rs_recv.at[phase, color, piece], device[axis])
+        return remote(src, recvs[phase].at[rs_slot(phase, color, piece)], rs_send.at[phase], recv_sem(rs_recv, phase, color, piece),
+                      device[axis])
+
+    def recv_sem(sems, phase, color, piece):
+        return sems.at[phase, color, min(piece, 2) if phase < 2 else 0]
+
+    def rs_arrive(phase, color, pieces):
+        first = pieces[0]
+        slot = rs_slot(phase, color, pl.ds(first, len(pieces)))
+        arrived(recvs[phase].at[slot], recv_sem(rs_recv, phase, color, first))
 
     def rs_add(phase, color, coord, rows, pieces):
         axis, fixed, cols = ctx(phase, color)
@@ -217,16 +222,15 @@
         own[idx] = total
 
     def rs_mid(phase, color):
-        rs_copy(phase, color, 0).wait_recv()
+        rs_arrive(phase, color, (0,))
         rs_add(phase, color, right, LO, (0,))
         rs_copy(phase, color, 4).start()
-        rs_copy(phase, color, 1).wait_recv()
+        rs_arrive(phase, color, (1,))
         rs_add(phase, color, left, HI, (1,))
         rs_copy(phase, color, 5).start()
 
     def rs_end(phase, color):
-        for piece in (2, 3, 4, 5):
-            rs_copy(phase, color, piece).wait_recv()
+        rs_arrive(phase, color, (2, 3, 4, 5))
         rs_add(phase, color, pos, LO, (3, 4))
         rs_add(phase, color, pos, HI, (2, 5))
 
@@ -260,8 +264,7 @@
                 rs_copy(2, color, piece).start()
     with jax.named_scope('rs2'):
         for color in range(3):
-            for piece in range(3):
-                rs_copy(2, color, piece).wait_recv()
+            rs_arrive(2, color, (0, 1, 2))
             rs_add(2, color, pos, ALL, range(3))
 
     @pl.when(core == ATTN)
@@ -302,7 +305,7 @@
         return place(x_all, {axis: coord[axis], second: pl.ds(2 * half, 2)}, ALL, pl.ds(*COLS[color]))
 
     def ag_remote(part, phase, color, piece, device):
-        return remote(part, part, ag_send.at[phase, color, piece], ag_recv.at[phase, color, piece], device[ORDER[color][phase]])
+        return remote(part, part, ag_send.at[phase], recv_sem(ag_recv, phase, color, piece), device[ORDER[color][phase]])
 
     def ag_copy(phase, color, piece):
         if phase < 2:
@@ -311,28 +314,27 @@
         return ag_remote(ag_part(phase, color, pos, ALL), phase, color, piece, DIRECT[piece][1])
 
     def ag_arrive(phase, color, piece):
-        if phase < 2:
+        sem = recv_sem(ag_recv, phase, color, piece)
+        if phase == 2:
+            arrived(ag_part(phase, color, [pl.ds(0, 3)] * 3, ALL), sem)
+        elif piece < 2:
             coord, half = AG_LAND[piece]
-            part = ag_half(phase, color, coord, half)
+            arrived(ag_half(phase, color, coord, half), sem)
+        elif phase == 1:
+            arrived(ag_part(phase, color, [pl.ds(0, 2)] * 3, ALL), sem)
         else:
-            part = ag_part(phase, color, AG_DIRECT[piece], ALL)
-        ag_remote(part, phase, color, piece, right_dev).wait_recv()
+            arrived(place(x_all, {ORDER[color][0]: pl.ds(0, 2)}, ALL, pl.ds(*COLS[color])), sem)
 
     def drain_push():
+        departed(peer, push_sem)
+
         @pl.when(core == ATTN)
         def _():
-            for turn_idx in range(SIDE):
-                for color in range(3):
-                    for copy in expert_copies(color, turn_idx, True):
-                        copy.wait_send()
             for copy in mom_from_attn():
                 copy.wait_send()
 
         @pl.when(core == EXPERT)
         def _():
-            for turn_idx in range(SIDE):
-                for color in range(3):
-                    attn_copy(color, turn_idx, True).wait_send()
             for copy in mom_from_expert():
                 copy.wait_send()
 
@@ -342,14 +344,14 @@
                 ag_copy(2, color, piece).start()
         drain_push()
         for color in range(3):
-            for piece in range(3):
-                ag_arrive(2, color, piece)
+            ag_arrive(2, color, 0)
             for piece in range(4):
                 ag_copy(1, color, piece).start()
-    def drain(phase, make):
-        for color in range(3):
-            for piece in range(6 if phase < 2 else 3):
-                make(phase, color, piece).wait_send()
+    def rs_drain(phase):
+        departed(recvs[phase], rs_send.at[phase])
+
+    def ag_drain(phase):
+        departed((x_all.at[pl.ds(0, 3)], full.at[0, pl.ds(0, 3)], full.at[0, 0, pl.ds(0, 3)])[phase], ag_send.at[phase])
 
     def ag_mid(phase):
         for color in range(3):
@@ -358,50 +360,80 @@
             ag_arrive(phase, color, 1)
             ag_copy(phase, color, 5).start()
 
-    def norm_copy(color, piece):
-        axis = ORDER[color][0]
-        part = norms.at[color, pos[axis]]
-        return remote(part, part, norm_send.at[color, piece], norm_recv.at[color, piece], DIRECT[piece][1][axis])
-
-    def norm_arrive(color, piece):
-        axis = ORDER[color][0]
-        part = norms.at[color, AG_DIRECT[piece][axis]]
-        remote(part, part, norm_send.at[color, piece], norm_recv.at[color, piece], right_dev[axis]).wait_recv()
-
-    def square_tile(plane, cols):
-        val = full[plane + (ALL, cols)].reshape(32, 8, cols.size)
+    def norm_copy(level, color, piece):
+        axis = ORDER[color][level]
+        part = norms.at[level, color, pos[axis]]
+        return remote(part, part, norm_send.at[level], norm_recv.at[level, color], DIRECT[piece][1][axis])
+
+    def norm_sum(level, color):
+        arrived(norms.at[level, color, pl.ds(0, 3)], norm_recv.at[level, color])
+        return sum(norms[level, color, j] for j in range(SIDE))
+
+    def norm_send_all(level, color):
+        for piece in range(3):
+            norm_copy(level, color, piece).start()
+
+    def square_tile(line, cols):
+        val = full[line + (ALL, cols)].reshape(8, 8, cols.size)
         val = jnp.sum(val * val, axis=0)
         return sum(val[:, k:k + 128] for k in range(0, cols.size, 128))
 
     def norm_start(color):
-        axis = ORDER[color][0]
-        plane = region({axis: pos[axis]}, ALL, ALL)[:3]
+        first_axis, second_axis, _ = ORDER[color]
+        line = region({first_axis: pos[first_axis], second_axis: pos[second_axis]}, ALL, ALL)[:3]
         first, width = COLS[color]
         west = max(0, min(NARROW - first, width))
         for side, (start, size) in enumerate(((first, west), (first + west, width - west))):
-            val = square_tile(plane, pl.ds(start, size)) if size else jnp.zeros((8, 128), F32)
-            norms[color, pos[axis], side] = val
-        for piece in range(3):
-            norm_copy(color, piece).start()
-
-    drain(1, rs_copy)
-    drain(2, ag_copy)
+            val = square_tile(line, pl.ds(start, size)) if size else jnp.zeros((8, 128), F32)
+            norms[1, color, pos[second_axis], side] = val
+        norm_send_all(1, color)
+
+    def result_copies(role, which):
+        if role == ATTN:
+            source = (full.at[mine], out_pk)[which]
+            pairs = ((source.at[HI], source.at[LO], (mo_attn, got_attn)[which]),)
+        else:
+            first = pl.multiple_of(lax.rem(chip, 8) * CHIP_ROWS, CHIP_ROWS)
+            ups = ((full.at[mine + (LO, WEST)], full.at[mine + (HI, WEST)]), (turn.at[pl.ds(first, 8)], turn.at[pl.ds(first + 8, 8)]))[which]
+            pairs = (ups + ((mo_up, got_up)[which],), (stay_down.at[which], send_down.at[which], (mo_down, got_down)[which]))
+        stay = [pltpu.make_async_copy(pair[0], pair[2], stay_sem.at[which, k]) for k, pair in enumerate(pairs)]
+        away = [remote(pair[1], pair[2], back_send.at[which, k], back_recv.at[which, k], partner) for k, pair in enumerate(pairs)]
+        return stay, away
+
+    def result_start(role, which):
+        stay, away = result_copies(role, which)
+        for copy in away + stay:
+            copy.start()
+
+    with jax.named_scope('ag1_start'):
+        for color in range(3):
+            norm_start(color)
+
+        @pl.when(core == ATTN)
+        def _():
+            result_start(ATTN, 0)
+
+        @pl.when(core == EXPERT)
+        def _():
+            for rows, cols in ((LO, WEST), (HI, EAST)):
+                down = full[mine + (rows, EAST)]
+                send_down[0, :, cols] = down[SIDE:]
+                stay_down[0, :, cols] = down[:SIDE]
+            result_start(EXPERT, 0)
+        rs_drain(1)
+        ag_drain(2)
     with jax.named_scope('ag1_mid'):
         ag_mid(1)
+        for color in range(3):
+            norms[0, color, pos[ORDER[color][0]]] = norm_sum(1, color)
+            norm_send_all(0, color)
+        rs_drain(0)
+        rs_drain(2)
     with jax.named_scope('ag1_end'):
         for color in range(3):
-            for piece in (2, 3, 4, 5):
-                ag_arrive(1, color, piece)
-            norm_start(color)
-    drain(0, rs_copy)
-    drain(2, rs_copy)
-    drain(1, ag_copy)
+            ag_arrive(1, color, 2)
     with jax.named_scope('norm'):
-        for color in range(3):
-            for piece in range(3):
-                norm_arrive(color, piece)
-        tiles = [norms[color, j] for color in range(3) for j in range(SIDE)]
-        total = jnp.sum(sum(tiles), axis=(1, 2), keepdims=True)
+        total = jnp.sum(norm_sum(0, 0) + norm_sum(0, 1) + norm_sum(0, 2), axis=(1, 2), keepdims=True)
         west, east = total[0], total[1]
         both = west + east
         west = jnp.where(core == ATTN, both, west)
@@ -420,43 +452,11 @@
         ag_mid(0)
     with jax.named_scope('ag0_end'):
         for color in range(3):
-            for piece in (2, 3, 4, 5):
-                ag_arrive(0, color, piece)
-    for color in range(3):
-        for piece in range(3):
-            norm_copy(color, piece).wait_send()
-    drain(0, ag_copy)
-
-    @pl.when(core == ATTN)
-    def _():
-        send_attn[...] = full[mine + (LO, ALL)]
-        mo_attn[...] = full[mine + (HI, ALL)]
-
-    @pl.when(core == EXPERT)
-    def _():
-        send_up[...] = full[mine + (HI, WEST)]
-        mo_up[...] = full[mine + (LO, WEST)]
-        for rows, cols in ((LO, WEST), (HI, EAST)):
-            down = full[mine + (rows, EAST)]
-            send_down[:, cols] = down[SIDE:]
-            mo_down[:, cols] = down[:SIDE]
-
-    def back_from_attn(base, out_attn):
-        return [remote(send_attn, out_attn, ex_send.at[base], ex_recv.at[base], partner)]
-
-    def back_from_expert(base, out_up, out_down):
-        return [remote(send_up, out_up, ex_send.at[base], ex_recv.at[base], partner),
-                remote(send_down, out_down, ex_send.at[base + 1], ex_recv.at[base + 1], partner)]
-
-    @pl.when(core == ATTN)
-    def _():
-        for copy in back_from_attn(2, mo_attn):
-            copy.start()
-
-    @pl.when(core == EXPERT)
-    def _():
-        for copy in back_from_expert(2, mo_up, mo_down):
-            copy.start()
+            ag_arrive(0, color, 2)
+    for level in range(2):
+        departed(norms.at[level, :, pl.ds(0, 3)], norm_send.at[level])
+    ag_drain(1)
+    ag_drain(0)
 
     def weighted(a_val, q_val):
         return (COEF_B * a_val.astype(F32) + COEF_C * q_val.astype(BF16).astype(F32)).astype(BF16)
@@ -502,14 +502,13 @@
         with jax.named_scope('steps'):
             lax.fori_loop(0, NS_STEPS - 1, step, 0)
             gram(0, WIDE)
-        rows = aligned(chip * CHIP_ROWS, CHIP_ROWS)
-        a_val = a_mat[rows, :]
-        b_val = weighted(a_val, jnp.dot(a_val, a_mat[...], preferred_element_type=F32))
-        out = advance(x_mat[rows, :], jnp.dot(b_val, x_mat[...], preferred_element_type=F32)).astype(F32)
-        back_from_attn(2, mo_attn)[0].wait_send()
-        send_attn[...] = out[:8]
-        got_attn[...] = out[8:]
-        back_from_attn(4, got_attn)[0].start()
+        with jax.named_scope('last'):
+            rows = aligned(chip * CHIP_ROWS, CHIP_ROWS)
+            a_val = a_mat[rows, :]
+            b_val = weighted(a_val, jnp.dot(a_val, a_mat[...], preferred_element_type=F32))
+            out = advance(x_mat[rows, :], jnp.dot(b_val, x_mat[...], preferred_element_type=F32)).astype(F32)
+            out_pk[...] = out
+            result_start(ATTN, 1)
 
     @pl.when(core == EXPERT)
     def _():
@@ -538,44 +537,32 @@
             lax.fori_loop(0, NS_STEPS - 1, step, 0)
             gram(0, NARROW)
             gram(NARROW, NARROW)
-        poly(0, NARROW)
-        cols = aligned(chip // 8 * 128, 128)
-        out_up = advance(x_mat[WEST, cols], jnp.dot(b_mat[WEST, WEST], x_mat[WEST, cols], preferred_element_type=F32))
-        turn[...] = jnp.transpose(out_up.astype(F32))
-        rows = aligned(NARROW + chip // 2 * CHIP_ROWS, CHIP_ROWS)
-        a_val = a_mat[rows, WEST]
-        b_val = weighted(a_val, jnp.dot(a_val, a_mat[EAST, WEST], preferred_element_type=F32))
-        both = advance(x_mat[rows, :], jnp.dot(b_val, x_mat[EAST, :], preferred_element_type=F32)).astype(F32)
-        out_down = jnp.where(lax.rem(chip, 2) == 0, both[:8], both[8:])
-        for copy in back_from_expert(2, mo_up, mo_down):
-            copy.wait_send()
-        first = pl.multiple_of(lax.rem(chip, 8) * CHIP_ROWS, CHIP_ROWS)
-        send_up[...] = turn[pl.ds(first + 8, 8), :]
-        got_up[...] = turn[pl.ds(first, 8), :]
-        send_down[...] = out_down[SIDE:]
-        got_down[...] = out_down[:SIDE]
-        for copy in back_from_expert(4, got_up, got_down):
-            copy.start()
-
-    @pl.when(core == ATTN)
-    def _():
-        for copy in back_from_expert(2, mo_up, mo_down) + back_from_expert(4, got_up, got_down):
-            copy.wait_recv()
-
-    @pl.when(core == EXPERT)
-    def _():
-        for copy in back_from_attn(2, mo_attn) + back_from_attn(4, got_attn):
-            copy.wait_recv()
-
-    @pl.when(core == ATTN)
-    def _():
-        for copy in back_from_attn(4, got_attn):
-            copy.wait_send()
-
-    @pl.when(core == EXPERT)
-    def _():
-        for copy in back_from_expert(4, got_up, got_down):
-            copy.wait_send()
+        with jax.named_scope('last'):
+            poly(0, NARROW)
+            cols = aligned(chip // 8 * 128, 128)
+            out_up = advance(x_mat[WEST, cols], jnp.dot(b_mat[WEST, WEST], x_mat[WEST, cols], preferred_element_type=F32))
+            turn[...] = jnp.transpose(out_up.astype(F32))
+            rows = aligned(NARROW + chip // 2 * CHIP_ROWS, CHIP_ROWS)
+            a_val = a_mat[rows, WEST]
+            b_val = weighted(a_val, jnp.dot(a_val, a_mat[EAST, WEST], preferred_element_type=F32))
+            both = advance(x_mat[rows, :], jnp.dot(b_val, x_mat[EAST, :], preferred_element_type=F32)).astype(F32)
+            out_down = jnp.where(lax.rem(chip, 2) == 0, both[:8], both[8:])
+            send_down[1] = out_down[SIDE:]
+            stay_down[1] = out_down[:SIDE]
+            result_start(EXPERT, 1)
+
+    with jax.named_scope('swap'):
+        for role, other in ((ATTN, EXPERT), (EXPERT, ATTN)):
+            @pl.when(core == role)
+            def _(role=role, other=other):
+                for which in range(2):
+                    stay, away = result_copies(role, which)
+                    for copy in stay:
+                        copy.wait()
+                    for copy in away:
+                        copy.wait_send()
+                    for copy in result_copies(other, which)[1]:
+                        copy.wait_recv()
 
 
 def finish(*refs):
@@ -604,22 +591,25 @@
             *[pltpu.VMEM((6,) + (SIDE,) * free + (8, WIDE), F32) for free in (2, 1)],
             pltpu.VMEM((3, CHIP_ROWS, WIDE), F32),
             pltpu.VMEM((CHIP_ROWS, WIDE), F32),
-            *[pltpu.VMEM(shape, F32) for shape in shapes * 3],
+            *[pltpu.VMEM(shape, F32) for shape in shapes * 2],
+            *[pltpu.VMEM((2, SIDE, WIDE), F32)] * 2,
+            pltpu.VMEM((CHIP_ROWS, WIDE), F32),
             *[pltpu.VMEM((WIDE, WIDE), BF16)] * 3,
             pltpu.VMEM((128, NARROW), F32),
-            pltpu.VMEM(BLOCK, BF16), pltpu.VMEM((3, SIDE, 2, 8, 128), F32), pltpu.VMEM((1, WIDE), F32),
-            *[sem((3, SIDE, 3))] * 3,
-            *[sem((3, 3, 6))] * 4,
-            *[sem((6,))] * 2,
+            pltpu.VMEM(BLOCK, BF16), pltpu.VMEM((2, 3, SIDE, 2, 8, 128), F32), pltpu.VMEM((1, WIDE), F32),
+            sem((3, SIDE)), sem, sem((3, SIDE)),
+            sem((3,)), sem((3, 3, 3)), sem((3,)), sem((3, 3, 3)),
+            *[sem((2,))] * 2,
+            *[sem((2, 2))] * 3,
             sem((2,)),
-            *[sem((3, 3))] * 2,
+            sem((2,)), sem((2, 3)),
             pltpu.SemaphoreType.REGULAR,
         ]
         result = pl.pallas_call(
             functools.partial(kernel, group_size),
             out_shape=[jax.ShapeDtypeStruct(shape, F32) for shape in shapes * 2],
             in_specs=[hbm] * 6,
-            out_specs=[vmem] * 6,
+            out_specs=[hbm] * 6,
             scratch_shapes=scratch,
             compiler_params=pltpu.CompilerParams(collective_id=0, has_side_effects=True, vmem_limit_bytes=60 * 1024 * 1024),
             name='muon',

time: 83 us -> 77.9 us (0.939)
  Pallas kernels: 82 us -> 77 us
    pallas_call x1, Pallas kernels: 80.4 us -> 75.5 us  [step_local(): pl.pallas_call(functools.partial(kernel, group_size), out_shape=[jax.Shap...]
where the time goes in v4:
time: 77.9 us; the launch traced here: 77.7 us
  Pallas kernels  77 us (99%)
    pallas_call x1, Pallas kernels, step_local(): pl.pallas_call(functools.partial(kernel, group_size), out_shape=[jax.Shap...  75.5 us
    pallas_call x1, Pallas kernels, step_local(): pl.pallas_call(finish, out_shape=outs, in_specs=[vmem] * 9, out_specs=[vm...  1.56 us

profile of v4, /device:TPU:1, one launch (start us, length us, event | category | flops | bytes accessed | tf_op | source)
XLA Modules:
  0.0 77.7 jit_solution(8468357146996873309)
XLA Ops:
  0.6 75.5 %muon.1 = (f32[8,1024]{1,0:T(8,128)}, f32[8,512]{1,0:T(8,128)}, f32[4,1024]{1,0:T(4,128)}, f32[8,1024]{1,0:T(8,128)}, f32[8,512]{1,0:T(8,128)}, /*index=5*/f32[4,1024]{1,0:T(4,128)}) custom-call(f32[4,4,4,16,1024]{4,3,2,1,0:T(8,128)} %bitcast.18, f32[4,4,4,16,512]{4,3,2,1,0:T(8,128)} %bitcast.19, f32[4,4,4,8,1024]{4,3,2,1,0:T(8,128)} %bitcast.20, ...), custom_call_target="tpu_custom_call" | custom-call | tf_op jit(solution)/shard_map/muon/pallas_call | solution.py:608
  76.1 1.6 %finish.1 = (f32[8,1024]{1,0:T(8,128)}, f32[8,1024]{1,0:T(8,128)}, bf16[8,1024]{1,0:T(8,128)(2,1)}, f32[8,512]{1,0:T(8,128)}, f32[8,512]{1,0:T(8,128)}, /*index=...) custom-call(f32[8,1024]{1,0:T(8,128)} %get-tuple-element.24.refs_0_, ...), custom_call_target="tpu_custom_call" | custom-call | tf_op jit(solution)/shard_map/finish/pallas_call | solution.py:619

commit v5 on v4

--- a/solution.py
+++ b/solution.py
@@ -97,27 +97,37 @@
         axis = ORDER[color][0]
         return axis, (far[axis], right[axis], left[axis], pos[axis])
 
-    def attn_copy(color, turn_idx, push):
+    PARTS = ((0, 0), (0, 1), (1, None), (2, None), (3, None))
+
+    def attn_copy(color, part, push):
+        turn_idx, half = PARTS[part]
+        rows = ALL if half is None else HALF[half]
         axis, coords = turns(color)
         cols = pl.ds(*COLS[color])
-        src = place(grad_attn, {axis: coords[turn_idx]}, ALL, cols)
+        src = place(grad_attn, {axis: coords[turn_idx]}, rows, cols)
         if push:
-            dst = place(peer, {axis: coords[turn_idx]}, ALL, cols)
-            return remote(src, dst, push_sem, pull_sem.at[color, turn_idx], partner)
-        dst = place(own, {axis: coords[turn_idx]}, ALL, cols)
-        return pltpu.make_async_copy(src, dst, load_sem.at[color, turn_idx])
-
-    def expert_copies(color, turn_idx, push):
+            dst = place(peer, {axis: coords[turn_idx]}, rows, cols)
+            return remote(src, dst, push_sem, pull_sem.at[color, part], partner)
+        dst = place(own, {axis: coords[turn_idx]}, rows, cols)
+        return pltpu.make_async_copy(src, dst, load_sem.at[color, part])
+
+    def expert_copies(color, part, push):
+        turn_idx, half = PARTS[part]
         axis, coords = turns(color)
         copies = []
         for source, col, width, rows, packed in PIECES[color]:
-            src = place(grad_up if source == 'up' else grad_down, {axis: coords[turn_idx]}, ALL, pl.ds(col, width))
+            from_rows = ALL
+            if half is not None and source == 'up':
+                from_rows = rows = HALF[half]
+            elif half is not None and rows is not HALF[half]:
+                continue
+            src = place(grad_up if source == 'up' else grad_down, {axis: coords[turn_idx]}, from_rows, pl.ds(col, width))
             target = peer if push else own
             dst = place(target, {axis: coords[turn_idx]}, rows, pl.ds(packed, width))
             if push:
-                copies.append(remote(src, dst, push_sem, pull_sem.at[color, turn_idx], partner))
+                copies.append(remote(src, dst, push_sem, pull_sem.at[color, part], partner))
             else:
-                copies.append(pltpu.make_async_copy(src, dst, load_sem.at[color, turn_idx]))
+                copies.append(pltpu.make_async_copy(src, dst, load_sem.at[color, part]))
         return copies
 
     def mom_from_attn():
@@ -137,9 +147,9 @@
 
     @pl.when(core == ATTN)
     def _():
-        for turn_idx in range(SIDE):
+        for part in range(len(PARTS)):
             for color in range(3):
-                attn_copy(color, turn_idx, False).start()
+                attn_copy(color, part, False).start()
         for copy in keep_copies(ATTN):
             copy.start()
 
@@ -150,23 +160,23 @@
     def _():
         for copy in mom_from_attn():
             copy.start()
-        for turn_idx in range(SIDE):
+        for part in range(len(PARTS)):
             for color in range(3):
-                for copy in expert_copies(color, turn_idx, True):
+                for copy in expert_copies(color, part, True):
                     copy.start()
 
     @pl.when(core == EXPERT)
     def _():
-        for turn_idx in range(SIDE):
+        for part in range(len(PARTS)):
             for color in range(3):
-                attn_copy(color, turn_idx, True).start()
+                attn_copy(color, part, True).start()
         for copy in mom_from_expert():
             copy.start()
         for copy in keep_copies(EXPERT):
             copy.start()
-        for turn_idx in range(SIDE):
+        for part in range(len(PARTS)):
             for color in range(3):
-                for copy in expert_copies(color, turn_idx, False):
+                for copy in expert_copies(color, part, False):
                     copy.start()
         with jax.named_scope('gate'):
             pl.semaphore_wait(gate, 1)
@@ -176,11 +186,12 @@
         def _():
             pl.semaphore_signal(gate, inc=1, device_id={'data': partner}, device_id_type=pl.DeviceIdType.MESH)
 
-    def chip_sum(color, turn_idx):
+    def chip_sum(color, part):
         axis, coords = turns(color)
-        idx = region({axis: coords[turn_idx]}, ALL, pl.ds(*COLS[color]))
-        pltpu.make_async_copy(own.at[idx], own.at[idx], load_sem.at[color, turn_idx]).wait()
-        arrived(peer.at[idx], pull_sem.at[color, turn_idx])
+        turn_idx, half = PARTS[part]
+        idx = region({axis: coords[turn_idx]}, ALL if half is None else HALF[half], pl.ds(*COLS[color]))
+        pltpu.make_async_copy(own.at[idx], own.at[idx], load_sem.at[color, part]).wait()
+        arrived(peer.at[idx], pull_sem.at[color, part])
         own[idx] = own[idx] + peer[idx]
 
     PAIRED = ((far, 0, right_dev), (far, 1, left_dev), (right, 1, right_dev), (left, 0, left_dev), (right, 0, right_dev), (left, 1, left_dev))
@@ -190,44 +201,51 @@
         order = ORDER[color]
         return order[phase], {order[k]: pos[order[k]] for k in range(phase)}, pl.ds(*COLS[color])
 
-    def rs_slot(phase, color, piece):
-        return (piece,) + (ALL,) * (2 - phase) + (ALL, pl.ds(*COLS[color]))
-
-    def rs_copy(phase, color, piece):
+    def rs_slot(phase, color, piece, sub=None):
+        free = [ALL] * (2 - phase)
+        if sub is not None:
+            free[0] = pl.ds(2 * sub, 2)
+        return (piece, *free, ALL, pl.ds(*COLS[color]))
+
+    def recv_sem(sems, phase, color, piece, sub):
+        return sems.at[phase, color, 4 if phase == 2 or piece > 1 else 2 * piece + (sub or 0)]
+
+    def rs_region(phase, color, coord, rows, sub):
         axis, fixed, cols = ctx(phase, color)
+        fixed = {**fixed, axis: coord[axis]}
+        if sub is not None:
+            fixed[min(k for k in range(3) if k != axis)] = pl.ds(2 * sub, 2)
+        return region(fixed, rows, cols)
+
+    def rs_copy(phase, color, piece, sub=None):
         if phase < 2:
             coord, half, device = PAIRED[piece]
             rows = HALF[half]
         else:
             coord, device = DIRECT[piece]
             rows = ALL
-        src = place(own, {**fixed, axis: coord[axis]}, rows, cols)
-        return remote(src, recvs[phase].at[rs_slot(phase, color, piece)], rs_send.at[phase], recv_sem(rs_recv, phase, color, piece),
-                      device[axis])
-
-    def recv_sem(sems, phase, color, piece):
-        return sems.at[phase, color, min(piece, 2) if phase < 2 else 0]
-
-    def rs_arrive(phase, color, pieces):
+        return remote(own.at[rs_region(phase, color, coord, rows, sub)], recvs[phase].at[rs_slot(phase, color, piece, sub)],
+                      rs_send.at[phase], recv_sem(rs_recv, phase, color, piece, sub), device[ORDER[color][phase]])
+
+    def rs_arrive(phase, color, pieces, sub=None):
         first = pieces[0]
-        slot = rs_slot(phase, color, pl.ds(first, len(pieces)))
-        arrived(recvs[phase].at[slot], recv_sem(rs_recv, phase, color, first))
-
-    def rs_add(phase, color, coord, rows, pieces):
-        axis, fixed, cols = ctx(phase, color)
-        idx = region({**fixed, axis: coord[axis]}, rows, cols)
+        slot = rs_slot(phase, color, pl.ds(first, len(pieces)), sub)
+        arrived(recvs[phase].at[slot], recv_sem(rs_recv, phase, color, first, sub))
+
+    def rs_add(phase, color, coord, rows, pieces, sub=None):
+        idx = rs_region(phase, color, coord, rows, sub)
         total = own[idx]
         for piece in pieces:
-            total = total + recvs[phase][rs_slot(phase, color, piece)]
+            total = total + recvs[phase][rs_slot(phase, color, piece, sub)]
         own[idx] = total
 
-    def rs_mid(phase, color):
-        rs_arrive(phase, color, (0,))
-        rs_add(phase, color, right, LO, (0,))
-        rs_copy(phase, color, 4).start()
-        rs_arrive(phase, color, (1,))
-        rs_add(phase, color, left, HI, (1,))
-        rs_copy(phase, color, 5).start()
+    def rs_mid(phase, color, sub=None):
+        rs_arrive(phase, color, (0,), sub)
+        rs_add(phase, color, right, LO, (0,), sub)
+        rs_copy(phase, color, 4, sub).start()
+        rs_arrive(phase, color, (1,), sub)
+        rs_add(phase, color, left, HI, (1,), sub)
+        rs_copy(phase, color, 5, sub).start()
 
     def rs_end(phase, color):
         rs_arrive(phase, color, (2, 3, 4, 5))
@@ -235,20 +253,22 @@
         rs_add(phase, color, pos, HI, (2, 5))
 
     with jax.named_scope('rs0_load'):
-        for color in range(3):
-            chip_sum(color, 0)
-            rs_copy(0, color, 0).start()
-            rs_copy(0, color, 1).start()
+        for half in range(2):
+            for color in range(3):
+                chip_sum(color, half)
+                for sub in range(2):
+                    rs_copy(0, color, half, sub).start()
+        for part in (2, 3):
+            for color in range(3):
+                chip_sum(color, part)
+                rs_copy(0, color, part).start()
+    with jax.named_scope('rs0_mid'):
+        for sub in range(2):
+            for color in range(3):
+                rs_mid(0, color, sub)
         open_gate()
-        for turn_idx in (1, 2):
-            for color in range(3):
-                chip_sum(color, turn_idx)
-                rs_copy(0, color, turn_idx + 1).start()
-    with jax.named_scope('rs0_mid'):
-        for color in range(3):
-            rs_mid(0, color)
-        for color in range(3):
-            chip_sum(color, 3)
+        for color in range(3):
+            chip_sum(color, 4)
     with jax.named_scope('rs0_end'):
         for color in range(3):
             rs_end(0, color)
@@ -298,28 +318,29 @@
         axis, fixed, cols = ctx(phase, color)
         return place(full, {**fixed, axis: coord[axis]}, rows, cols)
 
-    def ag_half(phase, color, coord, half):
+    def ag_half(phase, color, coord, half, sub=None):
         if phase == 1:
             return ag_part(phase, color, coord, HALF[half])
         axis, second, _ = ORDER[color]
-        return place(x_all, {axis: coord[axis], second: pl.ds(2 * half, 2)}, ALL, pl.ds(*COLS[color]))
-
-    def ag_remote(part, phase, color, piece, device):
-        return remote(part, part, ag_send.at[phase], recv_sem(ag_recv, phase, color, piece), device[ORDER[color][phase]])
-
-    def ag_copy(phase, color, piece):
+        span = pl.ds(2 * half, 2) if sub is None else pl.ds(2 * half + sub, 1)
+        return place(x_all, {axis: coord[axis], second: span}, ALL, pl.ds(*COLS[color]))
+
+    def ag_remote(part, phase, color, piece, device, sub=None):
+        return remote(part, part, ag_send.at[phase], recv_sem(ag_recv, phase, color, piece, sub), device[ORDER[color][phase]])
+
+    def ag_copy(phase, color, piece, sub=None):
         if phase < 2:
             coord, half, device = AG_SEND[piece]
-            return ag_remote(ag_half(phase, color, coord, half), phase, color, piece, device)
+            return ag_remote(ag_half(phase, color, coord, half, sub), phase, color, piece, device, sub)
         return ag_remote(ag_part(phase, color, pos, ALL), phase, color, piece, DIRECT[piece][1])
 
-    def ag_arrive(phase, color, piece):
-        sem = recv_sem(ag_recv, phase, color, piece)
+    def ag_arrive(phase, color, piece, sub=None):
+        sem = recv_sem(ag_recv, phase, color, piece, sub)
         if phase == 2:
             arrived(ag_part(phase, color, [pl.ds(0, 3)] * 3, ALL), sem)
         elif piece < 2:
             coord, half = AG_LAND[piece]
-            arrived(ag_half(phase, color, coord, half), sem)
+            arrived(ag_half(phase, color, coord, half, sub), sem)
         elif phase == 1:
             arrived(ag_part(phase, color, [pl.ds(0, 2)] * 3, ALL), sem)
         else:
@@ -338,27 +359,17 @@
             for copy in mom_from_expert():
                 copy.wait_send()
 
-    with jax.named_scope('ag2'):
-        for color in range(3):
-            for piece in range(3):
-                ag_copy(2, color, piece).start()
-        drain_push()
-        for color in range(3):
-            ag_arrive(2, color, 0)
-            for piece in range(4):
-                ag_copy(1, color, piece).start()
     def rs_drain(phase):
         departed(recvs[phase], rs_send.at[phase])
 
     def ag_drain(phase):
         departed((x_all.at[pl.ds(0, 3)], full.at[0, pl.ds(0, 3)], full.at[0, 0, pl.ds(0, 3)])[phase], ag_send.at[phase])
 
-    def ag_mid(phase):
-        for color in range(3):
-            ag_arrive(phase, color, 0)
-            ag_copy(phase, color, 4).start()
-            ag_arrive(phase, color, 1)
-            ag_copy(phase, color, 5).start()
+    def ag_mid(phase, sub=None):
+        for color in range(3):
+            for piece in range(2):
+                ag_arrive(phase, color, piece, sub)
+                ag_copy(phase, color, piece + 4, sub).start()
 
     def norm_copy(level, color, piece):
         axis = ORDER[color][level]
@@ -405,10 +416,19 @@
         for copy in away + stay:
             copy.start()
 
+    with jax.named_scope('ag2'):
+        for color in range(3):
+            for piece in range(3):
+                ag_copy(2, color, piece).start()
+        drain_push()
+        rs_drain(0)
+        for color in range(3):
+            ag_arrive(2, color, 0)
+            norm_start(color)
+            for piece in range(4):
+                ag_copy(1, color, piece).start()
+
     with jax.named_scope('ag1_start'):
-        for color in range(3):
-            norm_start(color)
-
         @pl.when(core == ATTN)
         def _():
             result_start(ATTN, 0)
@@ -423,11 +443,10 @@
         rs_drain(1)
         ag_drain(2)
     with jax.named_scope('ag1_mid'):
-        ag_mid(1)
         for color in range(3):
             norms[0, color, pos[ORDER[color][0]]] = norm_sum(1, color)
             norm_send_all(0, color)
-        rs_drain(0)
+        ag_mid(1)
         rs_drain(2)
     with jax.named_scope('ag1_end'):
         for color in range(3):
@@ -446,10 +465,14 @@
             axis, cols = ORDER[color][0], pl.ds(*COLS[color])
             idx = region({axis: pos[axis]}, ALL, cols)
             x_all[idx] = (full[idx] * scales[:, cols]).astype(BF16)
-            for piece in range(4):
+            for sub in range(2):
+                for piece in range(2):
+                    ag_copy(0, color, piece, sub).start()
+            for piece in (2, 3):
                 ag_copy(0, color, piece).start()
     with jax.named_scope('ag0_mid'):
-        ag_mid(0)
+        for sub in range(2):
+            ag_mid(0, sub)
     with jax.named_scope('ag0_end'):
         for color in range(3):
             ag_arrive(0, color, 2)
@@ -597,8 +620,8 @@
             *[pltpu.VMEM((WIDE, WIDE), BF16)] * 3,
             pltpu.VMEM((128, NARROW), F32),
             pltpu.VMEM(BLOCK, BF16), pltpu.VMEM((2, 3, SIDE, 2, 8, 128), F32), pltpu.VMEM((1, WIDE), F32),
-            sem((3, SIDE)), sem, sem((3, SIDE)),
-            sem((3,)), sem((3, 3, 3)), sem((3,)), sem((3, 3, 3)),
+            sem((3, 5)), sem, sem((3, 5)),
+            sem((3,)), sem((3, 3, 5)), sem((3,)), sem((3, 3, 5)),
             *[sem((2,))] * 2,
             *[sem((2, 2))] * 3,
             sem((2,)),

time: 77.9 us -> 76.4 us (0.981)
  Pallas kernels: 77 us -> 75.6 us
    pallas_call x1, Pallas kernels: 75.5 us -> 74.1 us  [step_local(): pl.pallas_call(functools.partial(kernel, group_size), out_shape=[jax.Shap...]
where the time goes in v5:
time: 76.4 us; the launch traced here: 76.3 us
  Pallas kernels  75.6 us (99%)
    pallas_call x1, Pallas kernels, step_local(): pl.pallas_call(functools.partial(kernel, group_size), out_shape=[jax.Shap...  74.1 us
    pallas_call x1, Pallas kernels, step_local(): pl.pallas_call(finish, out_shape=outs, in_specs=[vmem] * 9, out_specs=[vm...  1.56 us

profile of v5, /device:TPU:1, one launch (start us, length us, event | category | flops | bytes accessed | tf_op | source)
XLA Modules:
  0.0 76.3 jit_solution(4165048101434214566)
XLA Ops:
  0.6 74.1 %muon.1 = (f32[8,1024]{1,0:T(8,128)}, f32[8,512]{1,0:T(8,128)}, f32[4,1024]{1,0:T(4,128)}, f32[8,1024]{1,0:T(8,128)}, f32[8,512]{1,0:T(8,128)}, /*index=5*/f32[4,1024]{1,0:T(4,128)}) custom-call(f32[4,4,4,16,1024]{4,3,2,1,0:T(8,128)} %bitcast.18, f32[4,4,4,16,512]{4,3,2,1,0:T(8,128)} %bitcast.19, f32[4,4,4,8,1024]{4,3,2,1,0:T(8,128)} %bitcast.20, ...), custom_call_target="tpu_custom_call" | custom-call | tf_op jit(solution)/shard_map/muon/pallas_call | solution.py:631
  74.7 1.6 %finish.1 = (f32[8,1024]{1,0:T(8,128)}, f32[8,1024]{1,0:T(8,128)}, bf16[8,1024]{1,0:T(8,128)(2,1)}, f32[8,512]{1,0:T(8,128)}, f32[8,512]{1,0:T(8,128)}, /*index=...) custom-call(f32[8,1024]{1,0:T(8,128)} %get-tuple-element.24.refs_0_, ...), custom_call_target="tpu_custom_call" | custom-call | tf_op jit(solution)/shard_map/finish/pallas_call | solution.py:642

commit v6 on v5

--- a/solution.py
+++ b/solution.py
@@ -97,23 +97,23 @@
         axis = ORDER[color][0]
         return axis, (far[axis], right[axis], left[axis], pos[axis])
 
-    PARTS = ((0, 0), (0, 1), (1, None), (2, None), (3, None))
-
-    def attn_copy(color, part, push):
-        turn_idx, half = PARTS[part]
-        rows = ALL if half is None else HALF[half]
+    PARTS = ((0, 0, 0), (0, 1, 0), (0, 0, 1), (0, 1, 1), (1, None, None), (2, None, None), (3, None, None))
+
+    def turn_fixed(color, turn_idx, sub):
         axis, coords = turns(color)
-        cols = pl.ds(*COLS[color])
-        src = place(grad_attn, {axis: coords[turn_idx]}, rows, cols)
-        if push:
-            dst = place(peer, {axis: coords[turn_idx]}, rows, cols)
-            return remote(src, dst, push_sem, pull_sem.at[color, part], partner)
-        dst = place(own, {axis: coords[turn_idx]}, rows, cols)
-        return pltpu.make_async_copy(src, dst, load_sem.at[color, part])
-
-    def expert_copies(color, part, push):
-        turn_idx, half = PARTS[part]
-        axis, coords = turns(color)
+        fixed = {axis: coords[turn_idx]}
+        if sub is not None:
+            fixed[min(k for k in range(3) if k != axis)] = pl.ds(2 * sub, 2)
+        return fixed
+
+    def attn_copy(color, part):
+        turn_idx, half, sub = PARTS[part]
+        idx = region(turn_fixed(color, turn_idx, sub), ALL if half is None else HALF[half], pl.ds(*COLS[color]))
+        return remote(grad_attn.at[idx], peer.at[idx], push_sem, pull_sem.at[color, part], partner)
+
+    def expert_copies(color, part):
+        turn_idx, half, sub = PARTS[part]
+        fixed = turn_fixed(color, turn_idx, sub)
         copies = []
         for source, col, width, rows, packed in PIECES[color]:
             from_rows = ALL
@@ -121,13 +121,8 @@
                 from_rows = rows = HALF[half]
             elif half is not None and rows is not HALF[half]:
                 continue
-            src = place(grad_up if source == 'up' else grad_down, {axis: coords[turn_idx]}, from_rows, pl.ds(col, width))
-            target = peer if push else own
-            dst = place(target, {axis: coords[turn_idx]}, rows, pl.ds(packed, width))
-            if push:
-                copies.append(remote(src, dst, push_sem, pull_sem.at[color, part], partner))
-            else:
-                copies.append(pltpu.make_async_copy(src, dst, load_sem.at[color, part]))
+            src = place(grad_up if source == 'up' else grad_down, fixed, from_rows, pl.ds(col, width))
+            copies.append(remote(src, place(peer, fixed, rows, pl.ds(packed, width)), push_sem, pull_sem.at[color, part], partner))
         return copies
 
     def mom_from_attn():
@@ -147,9 +142,7 @@
 
     @pl.when(core == ATTN)
     def _():
-        for part in range(len(PARTS)):
-            for color in range(3):
-                attn_copy(color, part, False).start()
+        pltpu.make_async_copy(grad_attn, own, load_sem).start()
         for copy in keep_copies(ATTN):
             copy.start()
 
@@ -162,22 +155,20 @@
             copy.start()
         for part in range(len(PARTS)):
             for color in range(3):
-                for copy in expert_copies(color, part, True):
+                for copy in expert_copies(color, part):
                     copy.start()
 
     @pl.when(core == EXPERT)
     def _():
         for part in range(len(PARTS)):
             for color in range(3):
-                attn_copy(color, part, True).start()
+                attn_copy(color, part).start()
         for copy in mom_from_expert():
             copy.start()
         for copy in keep_copies(EXPERT):
             copy.start()
-        for part in range(len(PARTS)):
-            for color in range(3):
-                for copy in expert_copies(color, part, False):
-                    copy.start()
+        for src, rows, cols in ((grad_up, ALL, WEST), (grad_down.at[:, :, :, :, WEST], LO, EAST), (grad_down.at[:, :, :, :, EAST], HI, EAST)):
+            pltpu.make_async_copy(src, place(own, {}, rows, cols), load_sem).start()
         with jax.named_scope('gate'):
             pl.semaphore_wait(gate, 1)
 
@@ -187,10 +178,8 @@
             pl.semaphore_signal(gate, inc=1, device_id={'data': partner}, device_id_type=pl.DeviceIdType.MESH)
 
     def chip_sum(color, part):
-        axis, coords = turns(color)
-        turn_idx, half = PARTS[part]
-        idx = region({axis: coords[turn_idx]}, ALL if half is None else HALF[half], pl.ds(*COLS[color]))
-        pltpu.make_async_copy(own.at[idx], own.at[idx], load_sem.at[color, part]).wait()
+        turn_idx, half, sub = PARTS[part]
+        idx = region(turn_fixed(color, turn_idx, sub), ALL if half is None else HALF[half], pl.ds(*COLS[color]))
         arrived(peer.at[idx], pull_sem.at[color, part])
         own[idx] = own[idx] + peer[idx]
 
@@ -208,7 +197,11 @@
         return (piece, *free, ALL, pl.ds(*COLS[color]))
 
     def recv_sem(sems, phase, color, piece, sub):
-        return sems.at[phase, color, 4 if phase == 2 or piece > 1 else 2 * piece + (sub or 0)]
+        if phase == 2:
+            return sems.at[color]
+        if phase == 1:
+            return sems.at[3 + 3 * color + min(piece, 2)]
+        return sems.at[12 + 5 * color + (4 if piece > 1 else 2 * piece + sub)]
 
     def rs_region(phase, color, coord, rows, sub):
         axis, fixed, cols = ctx(phase, color)
@@ -253,22 +246,22 @@
         rs_add(phase, color, pos, HI, (2, 5))
 
     with jax.named_scope('rs0_load'):
-        for half in range(2):
-            for color in range(3):
-                chip_sum(color, half)
-                for sub in range(2):
-                    rs_copy(0, color, half, sub).start()
-        for part in (2, 3):
+        pltpu.make_async_copy(own, own, load_sem).wait()
+        for part in range(4):
             for color in range(3):
                 chip_sum(color, part)
-                rs_copy(0, color, part).start()
+                rs_copy(0, color, part % 2, part // 2).start()
+        for part in (4, 5):
+            for color in range(3):
+                chip_sum(color, part)
+                rs_copy(0, color, part - 2).start()
     with jax.named_scope('rs0_mid'):
         for sub in range(2):
             for color in range(3):
                 rs_mid(0, color, sub)
         open_gate()
         for color in range(3):
-            chip_sum(color, 4)
+            chip_sum(color, 6)
     with jax.named_scope('rs0_end'):
         for color in range(3):
             rs_end(0, color)
@@ -536,20 +529,15 @@
     @pl.when(core == EXPERT)
     def _():
         with jax.named_scope('fill'):
-            def fill_up(k, carry):
+            def fill(k, carry):
                 val = x_all[k // 2, pl.ds(2 * lax.rem(k, 2), 2), :, :, WEST].reshape(128, NARROW)
                 x_mat[WEST, aligned(k * 128, 128)] = jnp.transpose(val)
+                val = x_all[k // 2, pl.ds(2 * lax.rem(k, 2), 2), :, :, EAST].astype(F32)
+                rows = aligned(NARROW + k * 64, 64)
+                x_mat[rows, WEST] = val[:, :, :8].reshape(64, NARROW).astype(BF16)
+                x_mat[rows, EAST] = val[:, :, 8:].reshape(64, NARROW).astype(BF16)
                 return carry
-            lax.fori_loop(0, 8, fill_up, 0)
-
-            def fill_down(k, carry):
-                z, y, x = coords_of(2 * k)
-                val = x_all[z, y, pl.ds(x, 2), :, EAST].astype(F32)
-                rows = aligned(NARROW + k * CHIP_ROWS, CHIP_ROWS)
-                x_mat[rows, WEST] = val[:, :8].reshape(CHIP_ROWS, NARROW).astype(BF16)
-                x_mat[rows, EAST] = val[:, 8:].reshape(CHIP_ROWS, NARROW).astype(BF16)
-                return carry
-            lax.fori_loop(0, 32, fill_down, 0)
+            lax.fori_loop(0, 8, fill, 0)
 
         def step(_, carry):
             for stage in (gram, poly, update):
@@ -606,7 +594,8 @@
 
     def step_local(grad_attn, mom_attn, mas_attn, grad_up, mom_up, mas_up, grad_down, mom_down, mas_down):
         vmem = pl.BlockSpec(memory_space=pltpu.VMEM)
-        hbm = pl.BlockSpec(memory_space=pl.ANY)
+        hbm = pl.BlockSpec(memory_space=pltpu.HBM)
+        any_space = pl.BlockSpec(memory_space=pl.ANY)
         shapes = ((8, WIDE), (8, NARROW), (SIDE, WIDE))
         sem = pltpu.SemaphoreType.DMA
         scratch = [
@@ -620,8 +609,8 @@
             *[pltpu.VMEM((WIDE, WIDE), BF16)] * 3,
             pltpu.VMEM((128, NARROW), F32),
             pltpu.VMEM(BLOCK, BF16), pltpu.VMEM((2, 3, SIDE, 2, 8, 128), F32), pltpu.VMEM((1, WIDE), F32),
-            sem((3, 5)), sem, sem((3, 5)),
-            sem((3,)), sem((3, 3, 5)), sem((3,)), sem((3, 3, 5)),
+            sem, sem, sem((3, 7)),
+            sem((3,)), sem((27,)), sem((3,)), sem((27,)),
             *[sem((2,))] * 2,
             *[sem((2, 2))] * 3,
             sem((2,)),
@@ -632,14 +621,15 @@
             functools.partial(kernel, group_size),
             out_shape=[jax.ShapeDtypeStruct(shape, F32) for shape in shapes * 2],
             in_specs=[hbm] * 6,
-            out_specs=[hbm] * 6,
+            out_specs=[any_space] * 6,
             scratch_shapes=scratch,
-            compiler_params=pltpu.CompilerParams(collective_id=0, has_side_effects=True, vmem_limit_bytes=60 * 1024 * 1024),
+            compiler_params=pltpu.CompilerParams(collective_id=0, has_side_effects=True, vmem_limit_bytes=36 * 1024 * 1024),
             name='muon',
-        )(grad_attn.reshape(BLOCK), grad_up.reshape(BLOCK[:4] + (NARROW,)), grad_down.reshape(BLOCK[:3] + (8, WIDE)),
-          mom_attn[0], mom_up[0], mom_down[0])
+        )(*(pltpu.with_memory_space_constraint(v, pltpu.HBM) for v in (grad_attn.reshape(BLOCK), grad_up.reshape(BLOCK[:4] + (NARROW,)), grad_down.reshape(BLOCK[:3] + (8, WIDE)))),
+          *(pltpu.with_memory_space_constraint(v[0], pltpu.HBM) for v in (mom_attn, mom_up, mom_down)))
         outs = [jax.ShapeDtypeStruct(shape, dtype) for shape in shapes for dtype in (F32, F32, BF16)]
-        done = pl.pallas_call(finish, out_shape=outs, in_specs=[vmem] * 9, out_specs=[vmem] * 9, name='finish')(
+        done = pl.pallas_call(finish, out_shape=outs, in_specs=[vmem] * 9, out_specs=[vmem] * 9, name='finish',
+                              compiler_params=pltpu.CompilerParams(vmem_limit_bytes=4 * 1024 * 1024))(
             *result, mas_attn[0], mas_up[0], mas_down[0])
         return tuple(d[None] for d in done)
 

time: 76.4 us -> 75.1 us (0.983)
  Pallas kernels: 75.6 us -> 74.3 us
    pallas_call x1, Pallas kernels: 1.56 us -> 0.67 us  [step_local(): pl.pallas_call(finish, out_shape=outs, in_specs=[vmem] * 9, out_specs=[vm...]
where the time goes in v6:
time: 75.1 us; the launch traced here: 75 us
  Pallas kernels  74.3 us (99%)
    pallas_call x1, Pallas kernels, step_local(): pl.pallas_call(functools.partial(kernel, group_size), out_shape=[jax.Shap...  73.6 us

profile of v6, /device:TPU:1, one launch (start us, length us, event | category | flops | bytes accessed | tf_op | source)
XLA Modules:
  0.0 75.0 jit_solution(15978619697354532188)
XLA Ops:
  0.6 0.0 copy-start
  0.7 0.0 copy-start.1
  0.7 0.0 copy-start.2
  0.7 73.6 %muon.1 = (f32[8,1024]{1,0:T(8,128)S(1)}, f32[8,512]{1,0:T(8,128)S(1)}, f32[4,1024]{1,0:T(4,128)S(1)}, f32[8,1024]{1,0:T(8,128)S(1)}, f32[8,512]{1,0:T(8,128)S(1)}, /*index=5*/f32[4,1024]{1,0:T(4,128)S(1)}) custom-call(f32[4,4,4,16,1024]{4,3,2,1,0:T(8,128)} %bitcast.21, f32[4,4,4,16,512]{4,3,2,1,0:T(8,128)} %bitcast.22, f32[4,4,4,8,1024]{4,3,2,1,0:T(8,128)} %bitcast.23, ...), custom_call_target="tpu_custom_call" | custom-call | tf_op jit(solution)/shard_map/muon/pallas_call | solution.py:620
  74.3 0.0 copy-done
  74.3 0.0 copy-done.1
  74.3 0.0 copy-done.2
  74.3 0.7 finish.1
Async XLA Ops:
  0.6 73.7 %copy-start = (f32[1,8,1024]{2,1,0:T(8,128)S(1)}, f32[1,8,1024]{2,1,0:T(8,128)}, u32[]{:S(2)}) copy-start(f32[1,8,1024]{2,1,0:T(8,128)} %param.11) | copy-start | bytes 98308
  0.7 73.7 %copy-start.1 = (f32[1,8,512]{2,1,0:T(8,128)S(1)}, f32[1,8,512]{2,1,0:T(8,128)}, u32[]{:S(2)}) copy-start(f32[1,8,512]{2,1,0:T(8,128)} %param.14) | copy-start | bytes 49156
  0.7 73.7 %copy-start.2 = (f32[1,4,1024]{2,1,0:T(4,128)S(1)}, f32[1,4,1024]{2,1,0:T(4,128)}, u32[]{:S(2)}) copy-start(f32[1,4,1024]{2,1,0:T(4,128)} %param.17) | copy-start | bytes 49156

commit v7 on v6

--- a/solution.py
+++ b/solution.py
@@ -106,10 +106,13 @@
             fixed[min(k for k in range(3) if k != axis)] = pl.ds(2 * sub, 2)
         return fixed
 
+    def pull_of(color, part):
+        return pull_sem.at[3 * part + color if part < 4 else 8 + part]
+
     def attn_copy(color, part):
         turn_idx, half, sub = PARTS[part]
         idx = region(turn_fixed(color, turn_idx, sub), ALL if half is None else HALF[half], pl.ds(*COLS[color]))
-        return remote(grad_attn.at[idx], peer.at[idx], push_sem, pull_sem.at[color, part], partner)
+        return remote(grad_attn.at[idx], peer.at[idx], push_sem, pull_of(color, part), partner)
 
     def expert_copies(color, part):
         turn_idx, half, sub = PARTS[part]
@@ -122,19 +125,18 @@
             elif half is not None and rows is not HALF[half]:
                 continue
             src = place(grad_up if source == 'up' else grad_down, fixed, from_rows, pl.ds(col, width))
-            copies.append(remote(src, place(peer, fixed, rows, pl.ds(packed, width)), push_sem, pull_sem.at[color, part], partner))
+            copies.append(remote(src, place(peer, fixed, rows, pl.ds(packed, width)), push_sem, pull_of(color, part), partner))
         return copies
 
     def mom_from_attn():
-        return [remote(mom_up, swap_up, ex_send.at[0], ex_recv.at[0], partner),
-                remote(mom_down, swap_down, ex_send.at[1], ex_recv.at[1], partner)]
+        return [remote(mom_up, swap_up, ex_send, ex_recv, partner), remote(mom_down, swap_down, ex_send, ex_recv, partner)]
 
     def mom_from_expert():
-        return [remote(mom_attn, swap_attn, ex_send.at[0], ex_recv.at[0], partner)]
+        return [remote(mom_attn, swap_attn, ex_send, ex_recv, partner)]
 
     def keep_copies(role):
         pairs = ((mom_attn, keep_attn),) if role == ATTN else ((mom_up, keep_up), (mom_down, keep_down))
-        return [pltpu.make_async_copy(src, dst, keep_sem.at[k]) for k, (src, dst) in enumerate(pairs)]
+        return [pltpu.make_async_copy(src, dst, keep_sem) for src, dst in pairs]
 
     barrier = pltpu.get_barrier_semaphore()
     for device in [partner] + right_dev + left_dev:
@@ -180,7 +182,10 @@
     def chip_sum(color, part):
         turn_idx, half, sub = PARTS[part]
         idx = region(turn_fixed(color, turn_idx, sub), ALL if half is None else HALF[half], pl.ds(*COLS[color]))
-        arrived(peer.at[idx], pull_sem.at[color, part])
+        if part < 4:
+            arrived(peer.at[idx], pull_of(color, part))
+        elif color == 0:
+            arrived(peer.at[0], pull_of(color, part))
         own[idx] = own[idx] + peer[idx]
 
     PAIRED = ((far, 0, right_dev), (far, 1, left_dev), (right, 1, right_dev), (left, 0, left_dev), (right, 0, right_dev), (left, 1, left_dev))
@@ -259,9 +264,9 @@
         for sub in range(2):
             for color in range(3):
                 rs_mid(0, color, sub)
-        open_gate()
         for color in range(3):
             chip_sum(color, 6)
+    open_gate()
     with jax.named_scope('rs0_end'):
         for color in range(3):
             rs_end(0, color)
@@ -280,19 +285,16 @@
             rs_arrive(2, color, (0, 1, 2))
             rs_add(2, color, pos, ALL, range(3))
 
+    arrived(swap_attn, ex_recv)
+    pltpu.make_async_copy(keep_attn, keep_attn, keep_sem).wait()
+
     @pl.when(core == ATTN)
     def _():
-        mom_from_expert()[0].wait_recv()
-        keep_copies(ATTN)[0].wait()
         mom_pk[LO] = swap_attn[...]
         mom_pk[HI] = keep_attn[...]
 
     @pl.when(core == EXPERT)
     def _():
-        for copy in mom_from_attn():
-            copy.wait_recv()
-        for copy in keep_copies(EXPERT):
-            copy.wait()
         mom_pk[LO, WEST] = keep_up[...]
         mom_pk[HI, WEST] = swap_up[...]
         for first, cols in ((0, WEST), (8, EAST)):
@@ -341,16 +343,7 @@
 
     def drain_push():
         departed(peer, push_sem)
-
-        @pl.when(core == ATTN)
-        def _():
-            for copy in mom_from_attn():
-                copy.wait_send()
-
-        @pl.when(core == EXPERT)
-        def _():
-            for copy in mom_from_expert():
-                copy.wait_send()
+        departed(swap_attn, ex_send)
 
     def rs_drain(phase):
         departed(recvs[phase], rs_send.at[phase])
@@ -367,11 +360,13 @@
     def norm_copy(level, color, piece):
         axis = ORDER[color][level]
         part = norms.at[level, color, pos[axis]]
-        return remote(part, part, norm_send.at[level], norm_recv.at[level, color], DIRECT[piece][1][axis])
+        return remote(part, part, norm_send.at[level], norm_recv.at[level], DIRECT[piece][1][axis])
 
     def norm_sum(level, color):
-        arrived(norms.at[level, color, pl.ds(0, 3)], norm_recv.at[level, color])
         return sum(norms[level, color, j] for j in range(SIDE))
+
+    def norm_arrive(level):
+        arrived(norms.at[level, :, pl.ds(0, 3)], norm_recv.at[level])
 
     def norm_send_all(level, color):
         for piece in range(3):
@@ -400,8 +395,8 @@
             first = pl.multiple_of(lax.rem(chip, 8) * CHIP_ROWS, CHIP_ROWS)
             ups = ((full.at[mine + (LO, WEST)], full.at[mine + (HI, WEST)]), (turn.at[pl.ds(first, 8)], turn.at[pl.ds(first + 8, 8)]))[which]
             pairs = (ups + ((mo_up, got_up)[which],), (stay_down.at[which], send_down.at[which], (mo_down, got_down)[which]))
-        stay = [pltpu.make_async_copy(pair[0], pair[2], stay_sem.at[which, k]) for k, pair in enumerate(pairs)]
-        away = [remote(pair[1], pair[2], back_send.at[which, k], back_recv.at[which, k], partner) for k, pair in enumerate(pairs)]
+        stay = [pltpu.make_async_copy(pair[0], pair[2], stay_sem) for pair in pairs]
+        away = [remote(pair[1], pair[2], back_send, back_recv, partner) for pair in pairs]
         return stay, away
 
     def result_start(role, which):
@@ -436,6 +431,7 @@
         rs_drain(1)
         ag_drain(2)
     with jax.named_scope('ag1_mid'):
+        norm_arrive(1)
         for color in range(3):
             norms[0, color, pos[ORDER[color][0]]] = norm_sum(1, color)
             norm_send_all(0, color)
@@ -445,6 +441,7 @@
         for color in range(3):
             ag_arrive(1, color, 2)
     with jax.named_scope('norm'):
+        norm_arrive(0)
         total = jnp.sum(norm_sum(0, 0) + norm_sum(0, 1) + norm_sum(0, 2), axis=(1, 2), keepdims=True)
         west, east = total[0], total[1]
         both = west + east
@@ -510,13 +507,11 @@
         with jax.named_scope('fill'):
             x_mat[...] = x_all[...].reshape(WIDE, WIDE)
 
-        def step(_, carry):
-            gram(0, WIDE)
-            poly(0, WIDE)
-            update(0, WIDE)
-            return carry
         with jax.named_scope('steps'):
-            lax.fori_loop(0, NS_STEPS - 1, step, 0)
+            for _ in range(NS_STEPS - 1):
+                gram(0, WIDE)
+                poly(0, WIDE)
+                update(0, WIDE)
             gram(0, WIDE)
         with jax.named_scope('last'):
             rows = aligned(chip * CHIP_ROWS, CHIP_ROWS)
@@ -539,13 +534,11 @@
                 return carry
             lax.fori_loop(0, 8, fill, 0)
 
-        def step(_, carry):
-            for stage in (gram, poly, update):
-                stage(0, NARROW)
-                stage(NARROW, NARROW)
-            return carry
         with jax.named_scope('steps'):
-            lax.fori_loop(0, NS_STEPS - 1, step, 0)
+            for _ in range(NS_STEPS - 1):
+                for stage in (gram, poly, update):
+                    stage(0, NARROW)
+                    stage(NARROW, NARROW)
             gram(0, NARROW)
             gram(NARROW, NARROW)
         with jax.named_scope('last'):
@@ -563,17 +556,9 @@
             result_start(EXPERT, 1)
 
     with jax.named_scope('swap'):
-        for role, other in ((ATTN, EXPERT), (EXPERT, ATTN)):
-            @pl.when(core == role)
-            def _(role=role, other=other):
-                for which in range(2):
-                    stay, away = result_copies(role, which)
-                    for copy in stay:
-                        copy.wait()
-                    for copy in away:
-                        copy.wait_send()
-                    for copy in result_copies(other, which)[1]:
-                        copy.wait_recv()
+        pltpu.make_async_copy(out_pk, out_pk, stay_sem).wait()
+        departed(out_pk, back_send)
+        arrived(out_pk, back_recv)
 
 
 def finish(*refs):
@@ -609,12 +594,10 @@
             *[pltpu.VMEM((WIDE, WIDE), BF16)] * 3,
             pltpu.VMEM((128, NARROW), F32),
             pltpu.VMEM(BLOCK, BF16), pltpu.VMEM((2, 3, SIDE, 2, 8, 128), F32), pltpu.VMEM((1, WIDE), F32),
-            sem, sem, sem((3, 7)),
+            sem, sem, sem((15,)),
             sem((3,)), sem((27,)), sem((3,)), sem((27,)),
-            *[sem((2,))] * 2,
-            *[sem((2, 2))] * 3,
-            sem((2,)),
-            sem((2,)), sem((2, 3)),
+            *[sem] * 6,
+            sem((2,)), sem((2,)),
             pltpu.SemaphoreType.REGULAR,
         ]
         result = pl.pallas_call(

time: 75.1 us -> 74 us (0.985)
  Pallas kernels: 74.3 us -> 73.2 us
    pallas_call x1, Pallas kernels: 73.6 us -> 72.5 us  [step_local(): pl.pallas_call(functools.partial(kernel, group_size), out_shape=[jax.Shap...]
where the time goes in v7:
time: 74 us; the launch traced here: 73.9 us
  Pallas kernels  73.2 us (99%)
    pallas_call x1, Pallas kernels, step_local(): pl.pallas_call(functools.partial(kernel, group_size), out_shape=[jax.Shap...  72.5 us

profile of v7, /device:TPU:1, one launch (start us, length us, event | category | flops | bytes accessed | tf_op | source)
XLA Modules:
  0.0 73.9 jit_solution(6157426485480204187)
XLA Ops:
  0.6 0.0 copy-start
  0.7 0.0 copy-start.1
  0.7 0.0 copy-start.2
  0.7 72.5 %muon.1 = (f32[8,1024]{1,0:T(8,128)S(1)}, f32[8,512]{1,0:T(8,128)S(1)}, f32[4,1024]{1,0:T(4,128)S(1)}, f32[8,1024]{1,0:T(8,128)S(1)}, f32[8,512]{1,0:T(8,128)S(1)}, /*index=5*/f32[4,1024]{1,0:T(4,128)S(1)}) custom-call(f32[4,4,4,16,1024]{4,3,2,1,0:T(8,128)} %bitcast.21, f32[4,4,4,16,512]{4,3,2,1,0:T(8,128)} %bitcast.22, f32[4,4,4,8,1024]{4,3,2,1,0:T(8,128)} %bitcast.23, ...), custom_call_target="tpu_custom_call" | custom-call | tf_op jit(solution)/shard_map/muon/pallas_call | solution.py:603
  73.2 0.0 copy-done
  73.2 0.0 copy-done.1
  73.2 0.0 copy-done.2
  73.2 0.7 finish.1
Async XLA Ops:
  0.6 72.5 %copy-start = (f32[1,8,1024]{2,1,0:T(8,128)S(1)}, f32[1,8,1024]{2,1,0:T(8,128)}, u32[]{:S(2)}) copy-start(f32[1,8,1024]{2,1,0:T(8,128)} %param.11) | copy-start | bytes 98308
  0.7 72.5 %copy-start.1 = (f32[1,8,512]{2,1,0:T(8,128)S(1)}, f32[1,8,512]{2,1,0:T(8,128)}, u32[]{:S(2)}) copy-start(f32[1,8,512]{2,1,0:T(8,128)} %param.14) | copy-start | bytes 49156
  0.7 72.5 %copy-start.2 = (f32[1,4,1024]{2,1,0:T(4,128)S(1)}, f32[1,4,1024]{2,1,0:T(4,128)}, u32[]{:S(2)}) copy-start(f32[1,4,1024]{2,1,0:T(4,128)} %param.17) | copy-start | bytes 49156

commit v8 on v7

--- a/solution.py
+++ b/solution.py
@@ -171,8 +171,6 @@
             copy.start()
         for src, rows, cols in ((grad_up, ALL, WEST), (grad_down.at[:, :, :, :, WEST], LO, EAST), (grad_down.at[:, :, :, :, EAST], HI, EAST)):
             pltpu.make_async_copy(src, place(own, {}, rows, cols), load_sem).start()
-        with jax.named_scope('gate'):
-            pl.semaphore_wait(gate, 1)
 
     def open_gate():
         @pl.when(core == ATTN)
@@ -250,22 +248,36 @@
         rs_add(phase, color, pos, LO, (3, 4))
         rs_add(phase, color, pos, HI, (2, 5))
 
+    def attn_sum(color, part):
+        @pl.when(core == ATTN)
+        def _():
+            chip_sum(color, part)
+
     with jax.named_scope('rs0_load'):
         pltpu.make_async_copy(own, own, load_sem).wait()
+
+        @pl.when(core == EXPERT)
+        def _():
+            with jax.named_scope('gate'):
+                pl.semaphore_wait(gate, 1)
+            for part in range(len(PARTS)):
+                for color in range(3):
+                    chip_sum(color, part)
+
         for part in range(4):
             for color in range(3):
-                chip_sum(color, part)
+                attn_sum(color, part)
                 rs_copy(0, color, part % 2, part // 2).start()
         for part in (4, 5):
             for color in range(3):
-                chip_sum(color, part)
+                attn_sum(color, part)
                 rs_copy(0, color, part - 2).start()
     with jax.named_scope('rs0_mid'):
         for sub in range(2):
             for color in range(3):
                 rs_mid(0, color, sub)
         for color in range(3):
-            chip_sum(color, 6)
+            attn_sum(color, 6)
     open_gate()
     with jax.named_scope('rs0_end'):
         for color in range(3):
@@ -532,7 +544,7 @@
                 x_mat[rows, WEST] = val[:, :, :8].reshape(64, NARROW).astype(BF16)
                 x_mat[rows, EAST] = val[:, :, 8:].reshape(64, NARROW).astype(BF16)
                 return carry
-            lax.fori_loop(0, 8, fill, 0)
+            lax.fori_loop(0, 8, fill, 0, unroll=True)
 
         with jax.named_scope('steps'):
             for _ in range(NS_STEPS - 1):

time: 74 us -> 74 us (level)
  no operation moved by 1% of the time
where the time goes in v8:
time: 74 us; the launch traced here: 73.8 us
  Pallas kernels  73.1 us (99%)
    pallas_call x1, Pallas kernels, step_local(): pl.pallas_call(functools.partial(kernel, group_size), out_shape=[jax.Shap...  72.5 us

profile of v8, /device:TPU:1, one launch (start us, length us, event | category | flops | bytes accessed | tf_op | source)
XLA Modules:
  0.0 73.8 jit_solution(17101046848137613501)
XLA Ops:
  0.6 0.0 copy-start
  0.7 0.0 copy-start.1
  0.7 0.0 copy-start.2
  0.7 72.5 %muon.1 = (f32[8,1024]{1,0:T(8,128)S(1)}, f32[8,512]{1,0:T(8,128)S(1)}, f32[4,1024]{1,0:T(4,128)S(1)}, f32[8,1024]{1,0:T(8,128)S(1)}, f32[8,512]{1,0:T(8,128)S(1)}, /*index=5*/f32[4,1024]{1,0:T(4,128)S(1)}) custom-call(f32[4,4,4,16,1024]{4,3,2,1,0:T(8,128)} %bitcast.21, f32[4,4,4,16,512]{4,3,2,1,0:T(8,128)} %bitcast.22, f32[4,4,4,8,1024]{4,3,2,1,0:T(8,128)} %bitcast.23, ...), custom_call_target="tpu_custom_call" | custom-call | tf_op jit(solution)/shard_map/muon/pallas_call | solution.py:615
  73.1 0.0 copy-done
  73.1 0.0 copy-done.1
  73.2 0.0 copy-done.2
  73.2 0.7 finish.1
Async XLA Ops:
  0.6 72.5 %copy-start = (f32[1,8,1024]{2,1,0:T(8,128)S(1)}, f32[1,8,1024]{2,1,0:T(8,128)}, u32[]{:S(2)}) copy-start(f32[1,8,1024]{2,1,0:T(8,128)} %param.11) | copy-start | bytes 98308
  0.7 72.5 %copy-start.1 = (f32[1,8,512]{2,1,0:T(8,128)S(1)}, f32[1,8,512]{2,1,0:T(8,128)}, u32[]{:S(2)}) copy-start(f32[1,8,512]{2,1,0:T(8,128)} %param.14) | copy-start | bytes 49156
  0.7 72.5 %copy-start.2 = (f32[1,4,1024]{2,1,0:T(4,128)S(1)}, f32[1,4,1024]{2,1,0:T(4,128)}, u32[]{:S(2)}) copy-start(f32[1,4,1024]{2,1,0:T(4,128)} %param.17) | copy-start | bytes 49156
